TPU v7x, 256 devices: a 4x2x16 block of a 4x16x16 slice. The times are simulated.
256 devices in a mesh: group: 2 (over y), pool: 2 (over core), slab: 64 (over z, x).
Axes of the slice: x: 4, y: 2, z: 16, core: 2. Of those that a mesh axis runs over, the one named last changes fastest.
The devices are a block of a 4x16x16 slice.
Arguments:
- drho_part: float32 [2, 32, 2, 128, 128, 128], P('pool', 'group', None, 'slab'), parts along dimension 1, may hold values from -6 to 6
- fxc: float32 [128, 128, 128], P('slab'), may hold values from -2 to -0.2
- cutoff_mask: int32 [128, 128, 128], P(None, 'slab'), may hold values 0 or 1
- owner_table: int32 [32], P('group'), parts along dimension 0, may hold values from 0 to 15, each once
Outputs:
- dv: float32 [32, 2, 128, 128, 128], P('group', None, 'slab'), parts along dimension 0
There are 2 independent parts, one for each index of `group`. A program takes and returns all parts, laid end to end along the dimension named above; an argument that names none is the same for every part. Nothing has to cross between parts.
Inputs may be any that keep to these rules, and one draw needn't show every extreme that they name: `owner_table`: each perturbation appears in exactly one slot.
All inputs are finite; a program needn't handle non-finite values. No bound on the sum of `cutoff_mask` on one device may be relied on, other than what follows from the above.
Results may differ from a plain program's by a relative error of at most 0.00008.
Values sent between devices are 32-bit elements; how exact they have to be, the bound alone decides.
No kernel may reach another device: no remote copies, remote signals or barrier semaphores. Data moves between devices by JAX's collectives and lax.ppermute only.
A program may use at most 64 MiB of HBM per device.

v0:
```python
import functools
import math

import jax
import jax.numpy as jnp
import numpy as np
from jax import lax
from jax.experimental import pallas as pl
from jax.experimental.pallas import tpu as pltpu
from jax.sharding import PartitionSpec as P


F32 = jnp.float32
BF16 = jnp.bfloat16


def halves(table):
    high = table.astype(BF16)
    low = (table - high.astype(np.float64)).astype(BF16)
    return np.stack([high, low])


def dft(length, sign):
    index = np.arange(length)
    angle = 2.0 * np.pi * ((index[:, None] * index[None, :]) % length) / length
    cosine, sine = np.cos(angle), sign * np.sin(angle)
    return np.block([[cosine, -sine], [sine, cosine]])


def dealt_rows(length, devices, swap):
    width = length // devices
    rows = []
    for s in range(devices):
        s = s ^ 1 if swap else s
        rows += [r * length + s * width + b for r in range(2) for b in range(width)]
    return np.array(rows)


def dot3(left, right):
    dot = functools.partial(jnp.dot, preferred_element_type=F32)
    return dot(left[0], right[0]) + (dot(left[0], right[1]) + dot(left[1], right[0]))


def split(value):
    high = value.astype(BF16)
    return high, (value - high.astype(F32)).astype(BF16)


def gather(owner, start, local, kept, done, count):
    return [pltpu.make_async_copy(local.at[owner[start + k]], kept.at[k], done.at[k]) for k in range(count)]


def send_kernel(start, count, owner, pool, local, *rest):
    out, done = rest[-2:]
    copies = gather(owner, local.shape[0] // 2 * (1 - pool[0]) + start, local, out, done, count)
    for copy in copies:
        copy.start()
    for copy in copies:
        copy.wait()


def own_densities(start, count, owner, pool, local, kept, done):
    step = pl.program_id(0)
    copies = gather(owner, local.shape[0] // 2 * pool[0] + start, local, kept, done, count)

    @pl.when(step == 0)
    def _():
        for copy in copies:
            copy.start()

    for i in range(count // 2):

        @pl.when(step == i)
        def _():
            copies[2 * i].wait()
            copies[2 * i + 1].wait()


def forward_kernel(start, count, owner, pool, local, arrived, wz, wy, *rest):
    spectrum, kept, done = rest[-3:]
    n = kept.shape[-1]
    step = pl.program_id(0)
    own_densities(start, count, owner, pool, local, kept, done)
    mixed = []
    for k in range(2):
        x = kept[2 * step + k] + arrived[2 * step + k]
        rows = jnp.concatenate([x[0].reshape(2 * n, n), x[1].reshape(2 * n, n)], axis=1)
        y = dot3(split(rows), (wz[0], wz[1]))
        real = jnp.concatenate([y[:n, :n], y[n:, :n]], axis=1)
        imag = jnp.concatenate([y[:n, n:], y[n:, n:]], axis=1)
        stacked = split(jnp.concatenate([real, imag], axis=0))
        mixed.append(dot3((wy[k, 0], wy[k, 1]), stacked).reshape(-1, 8, 2 * n))
    even, odd = mixed
    lower = lax.broadcasted_iota(jnp.int32, even.shape, 1) < 4
    for j, value in enumerate((jnp.where(lower, even, odd), jnp.where(lower, odd, even))):
        for a in range(2):
            spectrum[:, j, a, 0] = value[:, :, a * n : (a + 1) * n]


def middle_kernel(columns, wx, wxi, kernel, out, rows, back):
    n = kernel.shape[-1]
    length = kernel.shape[1]
    step = pl.program_id(0)
    rows[...] = columns[:, step].reshape(rows.shape)
    grab = lambda j: rows[pl.ds(j, length, stride=8), :]
    order = [(p, b) for p in range(2) for b in range(2)]
    real = jnp.concatenate([grab(4 * p + b) for p, b in order], axis=1)
    imag = jnp.concatenate([grab(4 * p + 2 + b) for p, b in order], axis=1)
    spectrum = dot3((wx[0], wx[1]), split(jnp.concatenate([real, imag], axis=0)))
    both = jnp.concatenate([kernel[0], kernel[1]], axis=1)
    both = jnp.concatenate([both, both], axis=1)
    both = jnp.concatenate([both, both], axis=0)
    result = dot3((wxi[0], wxi[1]), split(spectrum * both))
    for i, (p, b) in enumerate(order):
        for r in range(2):
            back[pl.ds(4 * p + 2 * r + b, length, stride=8), :] = result[
                r * length : (r + 1) * length, i * n : (i + 1) * n
            ]
    out[:, step] = back[...].reshape(length, 8, n)


def backward_kernel(start, count, owner, pool, local, columns, wyi, wzi, fxc, arrived, *rest):
    own, sent, kept, done = rest[-4:]
    n = fxc.shape[-1]
    step = pl.program_id(0)
    own_densities(start, count, owner, pool, local, kept, done)
    place = start // 2 + step
    tiles = [jnp.concatenate([columns[:, j, a, place] for a in range(2)], axis=-1) for j in range(2)]
    lower = lax.broadcasted_iota(jnp.int32, tiles[0].shape, 1) < 4
    even = jnp.where(lower, tiles[0], tiles[1])
    odd = jnp.where(lower, tiles[1], tiles[0])
    for k, value in enumerate((even, odd)):
        y = dot3((wyi[k, 0], wyi[k, 1]), split(value.reshape(2 * n, 2 * n)))
        rows = jnp.concatenate(
            [
                jnp.concatenate([y[:n, a * n : (a + 1) * n], y[n:, a * n : (a + 1) * n]], axis=1)
                for a in range(2)
            ],
            axis=0,
        )
        x = dot3(split(rows), (wzi[0], wzi[1]))
        for r in range(2):
            part = x[:, r * n : (r + 1) * n].reshape(2, n, n)
            value = part + fxc[...] * (kept[2 * step + k, r] + arrived[2 * step + k, r])
            own[k, r] = value
            sent[2 * step + k, r] = value


def place_kernel(start, count, pool, arrived, kept, out, done):
    half = out.shape[0] // 2
    copy = pltpu.make_async_copy(arrived, out.at[pl.ds(half * (1 - pool[0]) + start, count)], done)
    copy.start()
    copy.wait()


def frequency(index, length):
    return ((index + length // 2) % length - length // 2).astype(F32)


def column_kernel(cutoff_mask, length):
    width = cutoff_mask.shape[1]
    start = lax.axis_index("slab") * width
    full_index = jnp.arange(length, dtype=jnp.int32)
    part_index = start + jnp.arange(width, dtype=jnp.int32)
    full_square = frequency(full_index, length) ** 2
    part_square = frequency(part_index, length) ** 2
    total = part_square[:, None, None] + full_square[None, :, None] + full_square[None, None, :]
    unit = (2.0 * math.pi / length) ** 2
    mask = jnp.swapaxes(cutoff_mask, 0, 1).astype(F32)
    scale = 1.0 / float(length) ** 3
    return (4.0 * math.pi * mask / (unit * total + 0.25)) * scale


RESIDENT = pl.BlockSpec(memory_space=pltpu.VMEM)


def taking(us):
    return pl.CostEstimate(flops=int(us * 1e8), bytes_accessed=0, transcendentals=0)


def per_device(drho_part, fxc, cutoff_mask, owner_table):
    local = drho_part[0]
    slots, _, planes, n, _ = local.shape
    devices = lax.axis_size("slab")
    mine = slots // 2
    tile = (2, planes, n, n)
    pool = lax.axis_index("pool").astype(jnp.int32).reshape(1)
    swap = [(0, 1), (1, 0)]
    limit = lambda share: pltpu.CompilerParams(vmem_limit_bytes=share << 20)
    ahead = [(0, 2), (2, mine - 2)]
    behind = ahead[::-1]

    forward = dft(n, -1.0)
    inverse = dft(n, 1.0)
    dealt = [dealt_rows(n, devices, s) for s in (False, True)]
    wz = jnp.asarray(halves(forward.T))
    wzi = jnp.asarray(halves(inverse.T))
    wy = jnp.asarray(np.stack([halves(forward[rows]) for rows in dealt]))
    wyi = jnp.asarray(np.stack([halves(inverse[:, rows]) for rows in dealt]))
    wx = jnp.asarray(halves(forward))
    wxi = jnp.asarray(halves(inverse))

    far = pl.BlockSpec(memory_space=pl.ANY)
    taken = lambda count: [pltpu.VMEM((count, *tile), F32), pltpu.SemaphoreType.DMA((count,))]

    arrived, sends = [], []
    for c, (start, count) in enumerate(ahead):
        sends.append(
            pl.pallas_call(
                functools.partial(send_kernel, start, count),
                out_shape=jax.ShapeDtypeStruct((count, *tile), F32),
                grid_spec=pltpu.PrefetchScalarGridSpec(
                    num_scalar_prefetch=2,
                    grid=(1,),
                    in_specs=[far] + [pl.BlockSpec(memory_space=pl.ANY)] * c,
                    out_specs=RESIDENT,
                    scratch_shapes=[pltpu.SemaphoreType.DMA((count,))],
                ),
                compiler_params=limit(54),
                cost_estimate=taking(0.7),
            )(owner_table, pool, local, *sends)
        )
        arrived.append(lax.ppermute(sends[-1], "pool", swap))

    shape = (devices // 2, 2, planes, mine // 2, 8, n)
    spectrum = None
    for c, (start, count) in enumerate(ahead):
        operands = [owner_table, pool, local, arrived[c], wz, wy]
        specs = [far, RESIDENT, RESIDENT, RESIDENT]
        aliases = {}
        if spectrum is not None:
            aliases = {len(operands): 0}
            operands.append(spectrum)
            specs.append(pl.BlockSpec(memory_space=pl.ANY))
        spectrum = pl.pallas_call(
            functools.partial(forward_kernel, start, count),
            out_shape=jax.ShapeDtypeStruct(shape, F32),
            grid_spec=pltpu.PrefetchScalarGridSpec(
                num_scalar_prefetch=2,
                grid=(count // 2,),
                in_specs=specs,
                out_specs=pl.BlockSpec(
                    (devices // 2, 2, planes, 1, 8, n), lambda i, *_, start=start: (0, 0, 0, start // 2 + i, 0, 0)
                ),
                scratch_shapes=taken(count),
            ),
            input_output_aliases=aliases,
            compiler_params=limit(40),
            cost_estimate=taking(0.8 * count),
        )(*operands)

    kernel = column_kernel(cutoff_mask, n)
    flat = (devices, planes * (mine // 2) * 8, n)
    columns = lax.all_to_all(spectrum.reshape(flat), "slab", split_axis=0, concat_axis=0, tiled=True)
    columns = columns.reshape(n, mine // 2, 8, n)
    columns = pl.pallas_call(
        middle_kernel,
        out_shape=jax.ShapeDtypeStruct(columns.shape, F32),
        grid=(mine // 2,),
        in_specs=[RESIDENT] * 4,
        out_specs=RESIDENT,
        scratch_shapes=[pltpu.VMEM((n * 8, n), F32), pltpu.VMEM((n * 8, n), F32)],
        compiler_params=limit(40),
        cost_estimate=taking(4),
        name="middle",
    )(columns, wx, wxi, kernel)
    columns = lax.all_to_all(columns.reshape(flat), "slab", split_axis=0, concat_axis=0, tiled=True)
    columns = columns.reshape(shape)

    out, others = None, []
    result = jax.ShapeDtypeStruct(local.shape, F32)
    for start, count in behind:
        operands = [owner_table, pool, local, columns, wyi, wzi, fxc, arrived[ahead.index((start, count))]]
        specs = [far] + [RESIDENT] * 5
        aliases = {}
        if out is not None:
            aliases = {len(operands): 0}
            operands.append(out)
            specs.append(pl.BlockSpec(memory_space=pl.ANY))
        out, sent = pl.pallas_call(
            functools.partial(backward_kernel, start, count),
            out_shape=(result, jax.ShapeDtypeStruct((count, *tile), F32)),
            grid_spec=pltpu.PrefetchScalarGridSpec(
                num_scalar_prefetch=2,
                grid=(count // 2,),
                in_specs=specs,
                out_specs=(
                    pl.BlockSpec(
                        (2, *tile), lambda i, own, q, start=start: (q[0] * (mine // 2) + start // 2 + i, 0, 0, 0, 0)
                    ),
                    RESIDENT,
                ),
                scratch_shapes=taken(count),
            ),
            input_output_aliases=aliases,
            compiler_params=limit(40),
            cost_estimate=taking(0.8 * count),
        )(*operands)
        others.append(lax.ppermute(sent, "pool", swap))
    for c, (start, count) in enumerate(behind):
        out = pl.pallas_call(
            functools.partial(place_kernel, start, count),
            out_shape=result,
            in_specs=[pl.BlockSpec(memory_space=pltpu.SMEM), RESIDENT, pl.BlockSpec(memory_space=pl.ANY)],
            out_specs=pl.BlockSpec(memory_space=pl.ANY),
            scratch_shapes=[pltpu.SemaphoreType.DMA],
            input_output_aliases={2: 0},
            compiler_params=limit(40),
            cost_estimate=taking(0.5),
        )(pool, others[c], out)
    return out


def solution(mesh):
    placed = (
        P("pool", "group", None, "slab", None, None),
        P("slab", None, None),
        P(None, "slab", None),
        P("group"),
    )

    return jax.shard_map(
        per_device,
        mesh=mesh,
        in_specs=placed,
        out_specs=P("group", None, "slab", None, None),
        check_vma=False,
    )
```

profile of v0, /device:TPU:33, one launch (start us, length us, event | category | flops | bytes accessed | tf_op | source)
XLA Modules:
  0.0 266.6 jit_solution(4031356163126798771)
XLA Ops:
  0.0 2.5 shard_map.100.rest_0_
  2.5 0.0 copy-start.5
  2.5 0.0 copy-start.7
  2.6 3.8 %shard_map.101 = f32[6,2,2,128,128]{4,3,2,1,0:T(8,128)} custom-call(s32[16]{0:T(128)} %owner.11, s32[1]{0:T(128)} %bitcast.pool, f32[16,2,2,128,128]{4,3,2,1,0:T(8,128)} %bitcast.11, f32[2,2,2,128,128]{4,3,2,1,0:T(8,128)} %shard_map.100.rest_0_), custom_call_target="tpu_custom_call" | custom-call | flops 70000000 | tf_op jit(solution)/shard_map/pallas_call | solution.py:209
  6.4 20.5 %collective-permute-start = (f32[6,2,2,128,128]{4,3,2,1,0:T(8,128)}, f32[6,2,2,128,128]{4,3,2,1,0:T(8,128)S(1)}, u32[]{:S(2)}, u32[]{:S(2)}) collective-permute-start(f32[6,2,2,128,128]{4,3,2,1,0:T(8,128)} %shard_map.101), channel_id=1, source_target_pairs={{0,64},{64,0},{1,65},{65,1},{2,66},{66,2},{3,67},{67,3},{4,68},{68... | collective-permute-start | bytes 4718600 | tf_op jit(solution)/shard_map/ppermute | solution.py:223
  26.9 0.2 collective-permute-start.1
  27.1 3.8 %collective-permute-done.1.arrived = f32[2,2,2,128,128]{4,3,2,1,0:T(8,128)S(1)} collective-permute-done((f32[2,2,2,128,128]{4,3,2,1,0:T(8,128)S(1)}, f32[2,2,2,128,128]{4,3,2,1,0:T(8,128)S(1)}, u32[]{:S(2)}, u32[]{:S(2)}) %collective-permute-start.1) | collective-permute-done | bytes 524320 | tf_op jit(solution)/shard_map/ppermute | solution.py:223
  30.9 2.3 shard_map.102.rest_0_
  33.2 4.3 %shard_map.103 = f32[32,2,2,4,8,128]{5,4,3,2,1,0:T(8,128)} custom-call(s32[16]{0:T(128)S(1)} %copy-done.9, s32[1]{0:T(128)} %bitcast.pool, f32[16,2,2,128,128]{4,3,2,1,0:T(8,128)S(1)} %bitcast.13, f32[6,2,2,128,128]{4,3,2,1,0:T(8,128)S(1)} %collective-permute-done.arrived, bf16[2,256,256]{2,1,0:T(8,128)(2,1)S(1)} %copy-done.5, ...), custom_call_target="tpu_custom_call", output_to_operand_aliasing={{}: (6, {})} | custom-call | flops 480000000 | tf_op jit(solution)/shard_map/pallas_call | solution.py:235
  37.6 0.0 copy-start.4
  37.6 9.9 %all-to-all-start = ((f32[64,64,128]{2,1,0:T(8,128)}), f32[64,64,128]{2,1,0:T(8,128)S(1)}, u32[]{:S(2)}, u32[]{:S(2)}) async-start(f32[64,64,128]{2,1,0:T(8,128)} %bitcast.2), calls=%async_computation | async-start | bytes 4194304 | tf_op jit(solution)/shard_map/all_to_all | solution.py:254
  47.5 0.1 broadcast_add_fusion
  47.6 0.1 fusion.kernel
  47.7 94.9 %all-to-all-done = f32[64,64,128]{2,1,0:T(8,128)S(1)} async-done(((f32[64,64,128]{2,1,0:T(8,128)}), f32[64,64,128]{2,1,0:T(8,128)S(1)}, u32[]{:S(2)}, u32[]{:S(2)}) %all-to-all-start) | async-done | bytes 2097184 | tf_op jit(solution)/shard_map/all_to_all | solution.py:254
  142.7 3.8 %middle.1 = f32[128,4,8,128]{3,2,1,0:T(8,128)S(1)} custom-call(f32[128,4,8,128]{3,2,1,0:T(8,128)S(1)} %bitcast.18, bf16[2,256,256]{2,1,0:T(8,128)(2,1)S(1)} %copy-done.4, bf16[2,256,256]{2,1,0:T(8,128)(2,1)S(1)} %copy-done.5, f32[2,128,128]{2,1,0:T(8,128)S(1)} %fusion.kernel), custom_call_target="tpu_custom_call" | custom-call | flops 400000000 | tf_op jit(solution)/shard_map/middle/pallas_call | solution.py:256
  146.4 103.9 %all_to_all.10 = f32[64,64,128]{2,1,0:T(8,128)S(1)} all-to-all(f32[64,64,128]{2,1,0:T(8,128)S(1)} %bitcast.19), channel_id=1, replica_groups=mesh['group'=2,'pool'=2,'slab'=64] {'slab'}, dimensions={0} | all-to-all | bytes 4194304 | tf_op jit(solution)/shard_map/all_to_all | solution.py:267
  250.3 4.3 %shard_map.104 = (f32[16,2,2,128,128]{4,3,2,1,0:T(8,128)}, f32[6,2,2,128,128]{4,3,2,1,0:T(8,128)S(1)}) custom-call(s32[16]{0:T(128)S(1)} %copy-done.9, s32[1]{0:T(128)} %bitcast.pool, f32[16,2,2,128,128]{4,3,2,1,0:T(8,128)S(1)} %bitcast.14, f32[32,2,2,4,8,128]{5,4,3,2,1,0:T(8,128)S(1)} %bitcast.16, bf16[2,2,256,256]{3,2,1,0:T(8,128)(2,1)S(1)} %copy-done.6, ...), custom_call_target="tpu_custom_call" | custom-call | flops 480000000 | tf_op jit(solution)/shard_map/pallas_call | solution.py:280
  254.6 6.8 %collective-permute-start.3 = (f32[6,2,2,128,128]{4,3,2,1,0:T(8,128)S(1)}, f32[6,2,2,128,128]{4,3,2,1,0:T(8,128)S(1)}, u32[]{:S(2)}, u32[]{:S(2)}) collective-permute-start(f32[6,2,2,128,128]{4,3,2,1,0:T(8,128)S(1)} %get-tuple-element.11), channel_id=1, source_target_pairs={{0,64},{64,0},{1,65},{65,1},{2,66},{66,2},{3,67},{67,3},{4,68},{68... | collective-permute-start | bytes 4718600 | tf_op jit(solution)/shard_map/ppermute | solution.py:299
  261.5 2.3 shard_map.105
  263.8 0.2 collective-permute-start.2
  264.0 0.6 collective-permute-done.3.arrived
  264.5 1.1 shard_map.106.kept
  265.7 0.2 collective-permute-done.2.arrived
  265.8 0.8 shard_map.107
  (24 shorter events, 0.1 us)
Async XLA Ops:
  2.5 24.4 %copy-start.10 = (f32[2,2,2,128,128]{4,3,2,1,0:T(8,128)S(1)}, f32[2,2,2,128,128]{4,3,2,1,0:T(8,128)}, u32[]{:S(2)}) copy-start(f32[2,2,2,128,128]{4,3,2,1,0:T(8,128)} %shard_map.100.rest_0_) | copy-start | bytes 1572868
  2.5 28.4 %copy-start = (f32[1,16,2,2,128,128]{5,4,3,2,1,0:T(8,128)S(1)}, f32[1,16,2,2,128,128]{5,4,3,2,1,0:T(8,128)}, u32[]{:S(2)}) copy-start(f32[1,16,2,2,128,128]{5,4,3,2,1,0:T(8,128)} %param.10) | copy-start | bytes 12582916
  2.5 28.4 %copy-start.5 = (bf16[2,256,256]{2,1,0:T(8,128)(2,1)S(1)}, bf16[2,256,256]{2,1,0:T(8,128)(2,1)}, u32[]{:S(2)}) copy-start(bf16[2,256,256]{2,1,0:T(8,128)(2,1)} %constant.58.clone.wz.wxi) | copy-start | bytes 786436
  2.5 28.4 %copy-start.7 = (bf16[2,2,256,256]{3,2,1,0:T(8,128)(2,1)S(1)}, bf16[2,2,256,256]{3,2,1,0:T(8,128)(2,1)}, u32[]{:S(2)}) copy-start(bf16[2,2,256,256]{3,2,1,0:T(8,128)(2,1)} %constant.60.clone.wy) | copy-start | bytes 1572868
  2.6 28.3 %copy-start.9 = (s32[16]{0:T(128)S(1)}, s32[16]{0:T(128)}, u32[]{:S(2)}) copy-start(s32[16]{0:T(128)} %owner.11) | copy-start | bytes 196
  6.4 26.9 %collective-permute-start = (f32[6,2,2,128,128]{4,3,2,1,0:T(8,128)}, f32[6,2,2,128,128]{4,3,2,1,0:T(8,128)S(1)}, u32[]{:S(2)}, u32[]{:S(2)}) collective-permute-start(f32[6,2,2,128,128]{4,3,2,1,0:T(8,128)} %shard_map.101), channel_id=1, source_target_pairs={{0,64},{64,0},{1,65},{65,1},{2,66},{66,2},{3,67},{67,3},{4,68},{68... | collective-permute-start | bytes 4718600 | tf_op jit(solution)/shard_map/ppermute | solution.py:223
  26.9 4.0 %collective-permute-start.1 = (f32[2,2,2,128,128]{4,3,2,1,0:T(8,128)S(1)}, f32[2,2,2,128,128]{4,3,2,1,0:T(8,128)S(1)}, u32[]{:S(2)}, u32[]{:S(2)}) collective-permute-start(f32[2,2,2,128,128]{4,3,2,1,0:T(8,128)S(1)} %copy-done.10), channel_id=1, source_target_pairs={{0,64},{64,0},{1,65},{65,1},{2,66},{66,2},{3,67},{67,3},{4,68},{68... | collective-permute-start | bytes 1572872 | tf_op jit(solution)/shard_map/ppermute | solution.py:223
  33.2 4.3 %copy-start.2 = (f32[6,2,2,128,128]{4,3,2,1,0:T(8,128)}, f32[6,2,2,128,128]{4,3,2,1,0:T(8,128)S(1)}, u32[]{:S(2)}) copy-start(f32[6,2,2,128,128]{4,3,2,1,0:T(8,128)S(1)} %collective-permute-done.arrived) | copy-start | bytes 4718596
  37.6 10.1 %copy-start.11 = (s32[128,2,128]{2,1,0:T(2,128)S(1)}, s32[128,2,128]{2,1,0:T(2,128)}, u32[]{:S(2)}) copy-start(s32[128,2,128]{2,1,0:T(2,128)} %param.12) | copy-start | bytes 393220
  37.6 105.1 %copy-start.4 = (bf16[2,256,256]{2,1,0:T(8,128)(2,1)S(1)}, bf16[2,256,256]{2,1,0:T(8,128)(2,1)}, u32[]{:S(2)}) copy-start(bf16[2,256,256]{2,1,0:T(8,128)(2,1)} %constant.59.clone.wx.wzi) | copy-start | bytes 786436
  37.6 105.1 %all-to-all-start = ((f32[64,64,128]{2,1,0:T(8,128)}), f32[64,64,128]{2,1,0:T(8,128)S(1)}, u32[]{:S(2)}, u32[]{:S(2)}) async-start(f32[64,64,128]{2,1,0:T(8,128)} %bitcast.2), calls=%async_computation | async-start | bytes 4194304 | tf_op jit(solution)/shard_map/all_to_all | solution.py:254
  142.7 107.7 %copy-start.3 = (f32[6,2,2,128,128]{4,3,2,1,0:T(8,128)S(1)}, f32[6,2,2,128,128]{4,3,2,1,0:T(8,128)}, u32[]{:S(2)}) copy-start(f32[6,2,2,128,128]{4,3,2,1,0:T(8,128)} %copy-done.2) | copy-start | bytes 4718596
  142.7 107.7 %copy-start.6 = (bf16[2,2,256,256]{3,2,1,0:T(8,128)(2,1)S(1)}, bf16[2,2,256,256]{3,2,1,0:T(8,128)(2,1)}, u32[]{:S(2)}) copy-start(bf16[2,2,256,256]{3,2,1,0:T(8,128)(2,1)} %constant.61.clone.wyi) | copy-start | bytes 1572868
  142.7 107.7 %copy-start.8 = (f32[2,128,128]{2,1,0:T(8,128)S(1)}, f32[2,128,128]{2,1,0:T(8,128)}, u32[]{:S(2)}) copy-start(f32[2,128,128]{2,1,0:T(8,128)} %fxc.3) | copy-start | bytes 393220
  146.4 103.9 %copy-start.1 = (f32[1,16,2,2,128,128]{5,4,3,2,1,0:T(8,128)S(1)}, f32[1,16,2,2,128,128]{5,4,3,2,1,0:T(8,128)}, u32[]{:S(2)}) copy-start(f32[1,16,2,2,128,128]{5,4,3,2,1,0:T(8,128)} %param.10) | copy-start | bytes 12582916
  254.6 9.9 %collective-permute-start.3 = (f32[6,2,2,128,128]{4,3,2,1,0:T(8,128)S(1)}, f32[6,2,2,128,128]{4,3,2,1,0:T(8,128)S(1)}, u32[]{:S(2)}, u32[]{:S(2)}) collective-permute-start(f32[6,2,2,128,128]{4,3,2,1,0:T(8,128)S(1)} %get-tuple-element.11), channel_id=1, source_target_pairs={{0,64},{64,0},{1,65},{65,1},{2,66},{66,2},{3,67},{67,3},{4,68},{68... | collective-permute-start | bytes 4718600 | tf_op jit(solution)/shard_map/ppermute | solution.py:299
  263.8 2.0 collective-permute-start.2
where the time goes:
time: 267 us
  blocking collectives  104 us (39%)
  waiting for transfers between devices  99.5 us (37%)
  starting transfers between devices  37.6 us (14%)
  Pallas kernels  25.2 us (9%)
    all_to_all x1, blocking collectives, per_device(): lax.all_to_all(columns.reshape(flat), 'slab', split_axis=0, concat_axis=0...  104 us
    all_to_all x1, waiting for transfers between devices, per_device(): lax.all_to_all(spectrum.reshape(flat), 'slab', split_axis=0, concat_axis=...  94.9 us
    ppermute x2, starting transfers between devices, per_device(): arrived.append(lax.ppermute(sends[-1], 'pool', swap))  20.7 us
    all_to_all x1, starting transfers between devices, per_device(): lax.all_to_all(spectrum.reshape(flat), 'slab', split_axis=0, concat_axis=...  9.92 us
    ppermute x2, starting transfers between devices, per_device(): others.append(lax.ppermute(sent, 'pool', swap))  6.98 us
    pallas_call x2, Pallas kernels, per_device(): pl.pallas_call(functools.partial(backward_kernel, start, count), out_shap...  6.63 us
    pallas_call x2, Pallas kernels, per_device(): pl.pallas_call(functools.partial(forward_kernel, start, count), out_shape...  6.59 us
    pallas_call x2, Pallas kernels, per_device(): pl.pallas_call(functools.partial(send_kernel, start, count), out_shape=ja...  6.29 us
  transfers between devices with their start and end apart: 5, of which 4 were waited for; matrix products, arithmetic and copies ran while one was open for 0% of the time, Pallas kernels for 2%

commit v1 on v0

--- a/solution.py
+++ b/solution.py
@@ -46,44 +46,26 @@
     return high, (value - high.astype(F32)).astype(BF16)
 
 
-def gather(owner, start, local, kept, done, count):
-    return [pltpu.make_async_copy(local.at[owner[start + k]], kept.at[k], done.at[k]) for k in range(count)]
-
-
-def send_kernel(start, count, owner, pool, local, *rest):
-    out, done = rest[-2:]
-    copies = gather(owner, local.shape[0] // 2 * (1 - pool[0]) + start, local, out, done, count)
+def collect_kernel(start, count, pool, local, *rest):
+    sent, own, done = rest[-3:]
+    half = local.shape[0] // 2
+    copies = [
+        pltpu.make_async_copy(local.at[pl.ds(half * q + start, count)], kept, done.at[k])
+        for k, (q, kept) in enumerate(((1 - pool[0], sent), (pool[0], own)))
+    ]
     for copy in copies:
         copy.start()
     for copy in copies:
         copy.wait()
 
 
-def own_densities(start, count, owner, pool, local, kept, done):
+def forward_kernel(own, arrived, wz, wy, *rest):
+    spectrum = rest[-1]
+    n = own.shape[-1]
     step = pl.program_id(0)
-    copies = gather(owner, local.shape[0] // 2 * pool[0] + start, local, kept, done, count)
-
-    @pl.when(step == 0)
-    def _():
-        for copy in copies:
-            copy.start()
-
-    for i in range(count // 2):
-
-        @pl.when(step == i)
-        def _():
-            copies[2 * i].wait()
-            copies[2 * i + 1].wait()
-
-
-def forward_kernel(start, count, owner, pool, local, arrived, wz, wy, *rest):
-    spectrum, kept, done = rest[-3:]
-    n = kept.shape[-1]
-    step = pl.program_id(0)
-    own_densities(start, count, owner, pool, local, kept, done)
     mixed = []
     for k in range(2):
-        x = kept[2 * step + k] + arrived[2 * step + k]
+        x = own[2 * step + k] + arrived[2 * step + k]
         rows = jnp.concatenate([x[0].reshape(2 * n, n), x[1].reshape(2 * n, n)], axis=1)
         y = dot3(split(rows), (wz[0], wz[1]))
         real = jnp.concatenate([y[:n, :n], y[n:, :n]], axis=1)
@@ -119,11 +101,9 @@
     out[:, step] = back[...].reshape(length, 8, n)
 
 
-def backward_kernel(start, count, owner, pool, local, columns, wyi, wzi, fxc, arrived, *rest):
-    own, sent, kept, done = rest[-4:]
+def backward_kernel(start, columns, wyi, wzi, fxc, own, arrived, out):
     n = fxc.shape[-1]
     step = pl.program_id(0)
-    own_densities(start, count, owner, pool, local, kept, done)
     place = start // 2 + step
     tiles = [jnp.concatenate([columns[:, j, a, place] for a in range(2)], axis=-1) for j in range(2)]
     lower = lax.broadcasted_iota(jnp.int32, tiles[0].shape, 1) < 4
@@ -141,16 +121,21 @@
         x = dot3(split(rows), (wzi[0], wzi[1]))
         for r in range(2):
             part = x[:, r * n : (r + 1) * n].reshape(2, n, n)
-            value = part + fxc[...] * (kept[2 * step + k, r] + arrived[2 * step + k, r])
-            own[k, r] = value
-            sent[2 * step + k, r] = value
-
-
-def place_kernel(start, count, pool, arrived, kept, out, done):
+            out[2 * step + k, r] = part + fxc[...] * (own[2 * step + k, r] + arrived[2 * step + k, r])
+
+
+def place_kernel(pieces, slot, pool, *rest):
+    parts, out, done = rest[: len(pieces)], rest[-2], rest[-1]
     half = out.shape[0] // 2
-    copy = pltpu.make_async_copy(arrived, out.at[pl.ds(half * (1 - pool[0]) + start, count)], done)
-    copy.start()
-    copy.wait()
+    copies = []
+    for (start, other), part in zip(pieces, parts):
+        first = half * (1 - pool[0] if other else pool[0]) + start
+        for k in range(part.shape[0]):
+            copies.append(pltpu.make_async_copy(part.at[k], out.at[slot[first + k]], done.at[len(copies)]))
+    for copy in copies:
+        copy.start()
+    for copy in copies:
+        copy.wait()
 
 
 def frequency(index, length):
@@ -201,55 +186,50 @@
     wxi = jnp.asarray(halves(inverse))
 
     far = pl.BlockSpec(memory_space=pl.ANY)
-    taken = lambda count: [pltpu.VMEM((count, *tile), F32), pltpu.SemaphoreType.DMA((count,))]
-
-    arrived, sends = [], []
+    scalars = pl.BlockSpec(memory_space=pltpu.SMEM)
+    parts = lambda count: jax.ShapeDtypeStruct((count, *tile), F32)
+
+    own, arrived, sends = [], [], []
     for c, (start, count) in enumerate(ahead):
-        sends.append(
-            pl.pallas_call(
-                functools.partial(send_kernel, start, count),
-                out_shape=jax.ShapeDtypeStruct((count, *tile), F32),
-                grid_spec=pltpu.PrefetchScalarGridSpec(
-                    num_scalar_prefetch=2,
-                    grid=(1,),
-                    in_specs=[far] + [pl.BlockSpec(memory_space=pl.ANY)] * c,
-                    out_specs=RESIDENT,
-                    scratch_shapes=[pltpu.SemaphoreType.DMA((count,))],
-                ),
-                compiler_params=limit(54),
-                cost_estimate=taking(0.7),
-            )(owner_table, pool, local, *sends)
-        )
-        arrived.append(lax.ppermute(sends[-1], "pool", swap))
+        sent, kept = pl.pallas_call(
+            functools.partial(collect_kernel, start, count),
+            out_shape=(parts(count), parts(count)),
+            in_specs=[scalars, far] + [far] * c,
+            out_specs=(RESIDENT, RESIDENT),
+            scratch_shapes=[pltpu.SemaphoreType.DMA((2,))],
+            compiler_params=limit(52 if c == 0 else 49),
+            cost_estimate=taking(1),
+        )(pool, local, *sends)
+        sends.append(sent)
+        own.append(kept)
+        arrived.append(lax.ppermute(sent, "pool", swap))
 
     shape = (devices // 2, 2, planes, mine // 2, 8, n)
     spectrum = None
     for c, (start, count) in enumerate(ahead):
-        operands = [owner_table, pool, local, arrived[c], wz, wy]
-        specs = [far, RESIDENT, RESIDENT, RESIDENT]
+        operands = [own[c], arrived[c], wz, wy]
+        specs = [RESIDENT] * 4
         aliases = {}
         if spectrum is not None:
             aliases = {len(operands): 0}
             operands.append(spectrum)
-            specs.append(pl.BlockSpec(memory_space=pl.ANY))
+            specs.append(far)
         spectrum = pl.pallas_call(
-            functools.partial(forward_kernel, start, count),
+            forward_kernel,
             out_shape=jax.ShapeDtypeStruct(shape, F32),
-            grid_spec=pltpu.PrefetchScalarGridSpec(
-                num_scalar_prefetch=2,
-                grid=(count // 2,),
-                in_specs=specs,
-                out_specs=pl.BlockSpec(
-                    (devices // 2, 2, planes, 1, 8, n), lambda i, *_, start=start: (0, 0, 0, start // 2 + i, 0, 0)
-                ),
-                scratch_shapes=taken(count),
+            grid=(count // 2,),
+            in_specs=specs,
+            out_specs=pl.BlockSpec(
+                (devices // 2, 2, planes, 1, 8, n), lambda i, start=start: (0, 0, 0, start // 2 + i, 0, 0)
             ),
             input_output_aliases=aliases,
             compiler_params=limit(40),
-            cost_estimate=taking(0.8 * count),
+            cost_estimate=taking(0.6 * count),
         )(*operands)
 
     kernel = column_kernel(cutoff_mask, n)
+    index = jnp.arange(slots, dtype=jnp.int32)
+    slot = jnp.sum(jnp.where(owner_table[None, :] == index[:, None], index[None, :], 0), axis=1)
     flat = (devices, planes * (mine // 2) * 8, n)
     columns = lax.all_to_all(spectrum.reshape(flat), "slab", split_axis=0, concat_axis=0, tiled=True)
     columns = columns.reshape(n, mine // 2, 8, n)
@@ -267,48 +247,39 @@
     columns = lax.all_to_all(columns.reshape(flat), "slab", split_axis=0, concat_axis=0, tiled=True)
     columns = columns.reshape(shape)
 
-    out, others = None, []
-    result = jax.ShapeDtypeStruct(local.shape, F32)
+    results, others = [], []
     for start, count in behind:
-        operands = [owner_table, pool, local, columns, wyi, wzi, fxc, arrived[ahead.index((start, count))]]
-        specs = [far] + [RESIDENT] * 5
-        aliases = {}
-        if out is not None:
-            aliases = {len(operands): 0}
-            operands.append(out)
-            specs.append(pl.BlockSpec(memory_space=pl.ANY))
-        out, sent = pl.pallas_call(
-            functools.partial(backward_kernel, start, count),
-            out_shape=(result, jax.ShapeDtypeStruct((count, *tile), F32)),
-            grid_spec=pltpu.PrefetchScalarGridSpec(
-                num_scalar_prefetch=2,
+        k = ahead.index((start, count))
+        results.append(
+            pl.pallas_call(
+                functools.partial(backward_kernel, start),
+                out_shape=parts(count),
                 grid=(count // 2,),
-                in_specs=specs,
-                out_specs=(
-                    pl.BlockSpec(
-                        (2, *tile), lambda i, own, q, start=start: (q[0] * (mine // 2) + start // 2 + i, 0, 0, 0, 0)
-                    ),
-                    RESIDENT,
-                ),
-                scratch_shapes=taken(count),
-            ),
+                in_specs=[RESIDENT] * 6,
+                out_specs=RESIDENT,
+                compiler_params=limit(40),
+                cost_estimate=taking(0.6 * count),
+            )(columns, wyi, wzi, fxc, own[k], arrived[k])
+        )
+        others.append(lax.ppermute(results[-1], "pool", swap))
+
+    def placed(pieces, arrays, out=None):
+        aliases = {} if out is None else {2 + len(arrays): 0}
+        kept = [] if out is None else [out]
+        return pl.pallas_call(
+            functools.partial(place_kernel, pieces),
+            out_shape=jax.ShapeDtypeStruct(local.shape, F32),
+            in_specs=[scalars, scalars] + [RESIDENT] * len(arrays) + [far] * len(kept),
+            out_specs=far,
+            scratch_shapes=[pltpu.SemaphoreType.DMA((sum(a.shape[0] for a in arrays),))],
             input_output_aliases=aliases,
             compiler_params=limit(40),
-            cost_estimate=taking(0.8 * count),
-        )(*operands)
-        others.append(lax.ppermute(sent, "pool", swap))
-    for c, (start, count) in enumerate(behind):
-        out = pl.pallas_call(
-            functools.partial(place_kernel, start, count),
-            out_shape=result,
-            in_specs=[pl.BlockSpec(memory_space=pltpu.SMEM), RESIDENT, pl.BlockSpec(memory_space=pl.ANY)],
-            out_specs=pl.BlockSpec(memory_space=pl.ANY),
-            scratch_shapes=[pltpu.SemaphoreType.DMA],
-            input_output_aliases={2: 0},
-            compiler_params=limit(40),
-            cost_estimate=taking(0.5),
-        )(pool, others[c], out)
-    return out
+            cost_estimate=taking(1),
+        )(slot, pool, *arrays, *kept)
+
+    starts = [start for start, _ in behind]
+    out = placed([(starts[0], False), (starts[1], False), (starts[0], True)], [*results, others[0]])
+    return placed([(starts[1], True)], [others[1]], out)
 
 
 def solution(mesh):

time: 267 us -> 262 us (0.981)
  Pallas kernels: 25.2 us -> 19.5 us
    pallas_call x8, Pallas kernels: 21.5 us -> 15.8 us  [the longest x2 5.2 us: per_device(): pl.pallas_call(forward_kernel, out_shape=jax.ShapeDtypeStruct(shape, F32)...]
  transfers between devices with their start and end apart: 5 -> 5, of which waited for: 4 -> 3; matrix products, arithmetic and copies ran while one was open for 0% -> 0% of each run, Pallas kernels for 2% -> 2%
where the time goes in v1:
time: 262 us
  blocking collectives  104 us (40%)
  waiting for transfers between devices  100 us (38%)
  starting transfers between devices  37.6 us (14%)
  Pallas kernels  19.5 us (7%)
    all_to_all x1, blocking collectives, per_device(): lax.all_to_all(columns.reshape(flat), 'slab', split_axis=0, concat_axis=0...  104 us
    all_to_all x1, waiting for transfers between devices, per_device(): lax.all_to_all(spectrum.reshape(flat), 'slab', split_axis=0, concat_axis=...  94.9 us
    ppermute x2, starting transfers between devices, per_device(): arrived.append(lax.ppermute(sent, 'pool', swap))  20.7 us
    all_to_all x1, starting transfers between devices, per_device(): lax.all_to_all(spectrum.reshape(flat), 'slab', split_axis=0, concat_axis=...  9.92 us
    ppermute x2, starting transfers between devices, per_device(): others.append(lax.ppermute(results[-1], 'pool', swap))  6.99 us
  transfers between devices with their start and end apart: 5, of which 3 were waited for; matrix products, arithmetic and copies ran while one was open for 0% of the time, Pallas kernels for 2%

profile of v1, /device:TPU:33, one launch (start us, length us, event | category | flops | bytes accessed | tf_op | source)
XLA Modules:
  0.0 262.0 jit_solution(6207002527443986783)
XLA Ops:
  0.0 1.2 shard_map.100
  1.2 0.0 copy-start.4
  1.2 0.0 copy-start.8
  1.2 2.0 shard_map.101
  3.2 20.5 %collective-permute-start = (f32[6,2,2,128,128]{4,3,2,1,0:T(8,128)S(1)}, f32[6,2,2,128,128]{4,3,2,1,0:T(8,128)S(1)}, u32[]{:S(2)}, u32[]{:S(2)}) collective-permute-start(f32[6,2,2,128,128]{4,3,2,1,0:T(8,128)S(1)} %get-tuple-element.11), channel_id=1, source_target_pairs={{0,64},{64,0},{1,65},{65,1},{2,66},{66,2},{3,67},{67,3},{4,68},{68... | collective-permute-start | bytes 4718600 | tf_op jit(solution)/shard_map/ppermute | solution.py:205
  23.8 0.1 collective-permute-start.1
  23.9 3.6 %collective-permute-done.1.arrived = f32[2,2,2,128,128]{4,3,2,1,0:T(8,128)S(1)} collective-permute-done((f32[2,2,2,128,128]{4,3,2,1,0:T(8,128)S(1)}, f32[2,2,2,128,128]{4,3,2,1,0:T(8,128)S(1)}, u32[]{:S(2)}, u32[]{:S(2)}) %collective-permute-start.1) | collective-permute-done | bytes 524320 | tf_op jit(solution)/shard_map/ppermute | solution.py:205
  27.6 1.7 shard_map.102.rest_0_
  29.3 3.5 %shard_map.103 = f32[32,2,2,4,8,128]{5,4,3,2,1,0:T(8,128)} custom-call(f32[6,2,2,128,128]{4,3,2,1,0:T(8,128)S(1)} %get-tuple-element.10.own, f32[6,2,2,128,128]{4,3,2,1,0:T(8,128)S(1)} %collective-permute-done.arrived, bf16[2,256,256]{2,1,0:T(8,128)(2,1)S(1)} %copy-done.4, bf16[2,2,256,256]{3,2,1,0:T(8,128)(2,1)S(1)} %copy-done.8, ...), custom_call_target="tpu_custom_call", output_to_operand_aliasing={{}: (4, {})} | custom-call | flops 360000000 | tf_op jit(solution)/shard_map/pallas_call | solution.py:217
  32.8 0.0 copy-start.5
  32.8 9.9 %all-to-all-start = ((f32[64,64,128]{2,1,0:T(8,128)}), f32[64,64,128]{2,1,0:T(8,128)S(1)}, u32[]{:S(2)}, u32[]{:S(2)}) async-start(f32[64,64,128]{2,1,0:T(8,128)} %bitcast.2), calls=%async_computation | async-start | bytes 4194304 | tf_op jit(solution)/shard_map/all_to_all | solution.py:234
  42.8 0.1 broadcast_add_fusion
  42.8 0.1 fusion.kernel
  43.0 94.9 %all-to-all-done = f32[64,64,128]{2,1,0:T(8,128)S(1)} async-done(((f32[64,64,128]{2,1,0:T(8,128)}), f32[64,64,128]{2,1,0:T(8,128)S(1)}, u32[]{:S(2)}, u32[]{:S(2)}) %all-to-all-start) | async-done | bytes 2097184 | tf_op jit(solution)/shard_map/all_to_all | solution.py:234
  137.9 3.7 %middle.1 = f32[128,4,8,128]{3,2,1,0:T(8,128)S(1)} custom-call(f32[128,4,8,128]{3,2,1,0:T(8,128)S(1)} %bitcast.12, bf16[2,256,256]{2,1,0:T(8,128)(2,1)S(1)} %copy-done.5, bf16[2,256,256]{2,1,0:T(8,128)(2,1)S(1)} %copy-done.4, f32[2,128,128]{2,1,0:T(8,128)S(1)} %fusion.kernel), custom_call_target="tpu_custom_call" | custom-call | flops 400000000 | tf_op jit(solution)/shard_map/middle/pallas_call | solution.py:236
  141.7 103.9 %all_to_all.10 = f32[64,64,128]{2,1,0:T(8,128)S(1)} all-to-all(f32[64,64,128]{2,1,0:T(8,128)S(1)} %bitcast.13), channel_id=1, replica_groups=mesh['group'=2,'pool'=2,'slab'=64] {'slab'}, dimensions={0} | all-to-all | bytes 4194304 | tf_op jit(solution)/shard_map/all_to_all | solution.py:247
  245.6 2.7 %shard_map.105.rest_0_ = f32[6,2,2,128,128]{4,3,2,1,0:T(8,128)S(1)} custom-call(f32[32,2,2,4,8,128]{5,4,3,2,1,0:T(8,128)S(1)} %bitcast.10, bf16[2,2,256,256]{3,2,1,0:T(8,128)(2,1)S(1)} %copy-done.9, bf16[2,256,256]{2,1,0:T(8,128)(2,1)S(1)} %copy-done.5, f32[2,128,128]{2,1,0:T(8,128)S(1)} %copy-done.10, f32[6,2,2,128,128]{4,3,2,1,0:T(8,128)S(1)} %copy-done.1, ...), custom_call_target="tpu_custom_call" | custom-call | flops 360000000 | tf_op jit(solution)/shard_map/pallas_call | solution.py:254
  248.3 6.8 %collective-permute-start.3 = (f32[6,2,2,128,128]{4,3,2,1,0:T(8,128)S(1)}, f32[6,2,2,128,128]{4,3,2,1,0:T(8,128)S(1)}, u32[]{:S(2)}, u32[]{:S(2)}) collective-permute-start(f32[6,2,2,128,128]{4,3,2,1,0:T(8,128)S(1)} %shard_map.105.rest_0_), channel_id=1, source_target_pairs={{0,64},{64,0},{1,65},{65,1},{2,66},{66,2},{3,67},{67,3},{4,68},{68... | collective-permute-start | bytes 4718600 | tf_op jit(solution)/shard_map/ppermute | solution.py:264
  255.1 0.9 shard_map.104.rest_1_
  256.0 0.2 collective-permute-start.2
  256.2 0.1 select_reduce_fusion.slot
  256.3 1.9 collective-permute-done.3.rest_2_
  258.1 2.5 shard_map.106.rest_1_
  260.6 1.4 shard_map.107
  (27 shorter events, 0.1 us)
Async XLA Ops:
  1.2 26.3 %copy-start.4 = (bf16[2,256,256]{2,1,0:T(8,128)(2,1)S(1)}, bf16[2,256,256]{2,1,0:T(8,128)(2,1)}, u32[]{:S(2)}) copy-start(bf16[2,256,256]{2,1,0:T(8,128)(2,1)} %constant.59.clone.wz.wxi) | copy-start | bytes 786436
  1.2 26.3 %copy-start.8 = (bf16[2,2,256,256]{3,2,1,0:T(8,128)(2,1)S(1)}, bf16[2,2,256,256]{3,2,1,0:T(8,128)(2,1)}, u32[]{:S(2)}) copy-start(bf16[2,2,256,256]{3,2,1,0:T(8,128)(2,1)} %constant.61.clone.wy) | copy-start | bytes 1572868
  3.2 29.5 %copy-start = (f32[6,2,2,128,128]{4,3,2,1,0:T(8,128)}, f32[6,2,2,128,128]{4,3,2,1,0:T(8,128)S(1)}, u32[]{:S(2)}) copy-start(f32[6,2,2,128,128]{4,3,2,1,0:T(8,128)S(1)} %get-tuple-element.10.own) | copy-start | bytes 4718596
  3.2 26.0 %collective-permute-start = (f32[6,2,2,128,128]{4,3,2,1,0:T(8,128)S(1)}, f32[6,2,2,128,128]{4,3,2,1,0:T(8,128)S(1)}, u32[]{:S(2)}, u32[]{:S(2)}) collective-permute-start(f32[6,2,2,128,128]{4,3,2,1,0:T(8,128)S(1)} %get-tuple-element.11), channel_id=1, source_target_pairs={{0,64},{64,0},{1,65},{65,1},{2,66},{66,2},{3,67},{67,3},{4,68},{68... | collective-permute-start | bytes 4718600 | tf_op jit(solution)/shard_map/ppermute | solution.py:205
  23.8 3.8 %collective-permute-start.1 = (f32[2,2,2,128,128]{4,3,2,1,0:T(8,128)S(1)}, f32[2,2,2,128,128]{4,3,2,1,0:T(8,128)S(1)}, u32[]{:S(2)}, u32[]{:S(2)}) collective-permute-start(f32[2,2,2,128,128]{4,3,2,1,0:T(8,128)S(1)} %get-tuple-element.9.rest_0_), channel_id=1, source_target_pairs={{0,64},{64,0},{1,65},{65,1},{2,66},{66,2},{3,67},{67,3},{4,68},{68... | collective-permute-start | bytes 1572872 | tf_op jit(solution)/shard_map/ppermute | solution.py:205
  27.6 5.2 %copy-start.6 = (f32[2,2,2,128,128]{4,3,2,1,0:T(8,128)}, f32[2,2,2,128,128]{4,3,2,1,0:T(8,128)S(1)}, u32[]{:S(2)}) copy-start(f32[2,2,2,128,128]{4,3,2,1,0:T(8,128)S(1)} %collective-permute-done.1.arrived) | copy-start | bytes 1572868
  29.3 3.5 %copy-start.2 = (f32[6,2,2,128,128]{4,3,2,1,0:T(8,128)}, f32[6,2,2,128,128]{4,3,2,1,0:T(8,128)S(1)}, u32[]{:S(2)}) copy-start(f32[6,2,2,128,128]{4,3,2,1,0:T(8,128)S(1)} %collective-permute-done.arrived) | copy-start | bytes 4718596
  32.8 10.1 %copy-start.11 = (s32[128,2,128]{2,1,0:T(2,128)S(1)}, s32[128,2,128]{2,1,0:T(2,128)}, u32[]{:S(2)}) copy-start(s32[128,2,128]{2,1,0:T(2,128)} %param.12) | copy-start | bytes 393220
  32.8 105.1 %copy-start.5 = (bf16[2,256,256]{2,1,0:T(8,128)(2,1)S(1)}, bf16[2,256,256]{2,1,0:T(8,128)(2,1)}, u32[]{:S(2)}) copy-start(bf16[2,256,256]{2,1,0:T(8,128)(2,1)} %constant.60.clone.wx.wzi) | copy-start | bytes 786436
  32.8 105.1 %all-to-all-start = ((f32[64,64,128]{2,1,0:T(8,128)}), f32[64,64,128]{2,1,0:T(8,128)S(1)}, u32[]{:S(2)}, u32[]{:S(2)}) async-start(f32[64,64,128]{2,1,0:T(8,128)} %bitcast.2), calls=%async_computation | async-start | bytes 4194304 | tf_op jit(solution)/shard_map/all_to_all | solution.py:234
  141.6 103.9 %copy-start.1 = (f32[6,2,2,128,128]{4,3,2,1,0:T(8,128)S(1)}, f32[6,2,2,128,128]{4,3,2,1,0:T(8,128)}, u32[]{:S(2)}) copy-start(f32[6,2,2,128,128]{4,3,2,1,0:T(8,128)} %copy-done) | copy-start | bytes 4718596
  141.6 103.9 %copy-start.3 = (f32[6,2,2,128,128]{4,3,2,1,0:T(8,128)S(1)}, f32[6,2,2,128,128]{4,3,2,1,0:T(8,128)}, u32[]{:S(2)}) copy-start(f32[6,2,2,128,128]{4,3,2,1,0:T(8,128)} %copy-done.2) | copy-start | bytes 4718596
  141.6 103.9 %copy-start.9 = (bf16[2,2,256,256]{3,2,1,0:T(8,128)(2,1)S(1)}, bf16[2,2,256,256]{3,2,1,0:T(8,128)(2,1)}, u32[]{:S(2)}) copy-start(bf16[2,2,256,256]{3,2,1,0:T(8,128)(2,1)} %constant.62.clone.wyi) | copy-start | bytes 1572868
  141.7 103.9 %copy-start.10 = (f32[2,128,128]{2,1,0:T(8,128)S(1)}, f32[2,128,128]{2,1,0:T(8,128)}, u32[]{:S(2)}) copy-start(f32[2,128,128]{2,1,0:T(8,128)} %fxc.3) | copy-start | bytes 393220
  245.5 9.6 %copy-start.7 = (f32[2,2,2,128,128]{4,3,2,1,0:T(8,128)S(1)}, f32[2,2,2,128,128]{4,3,2,1,0:T(8,128)}, u32[]{:S(2)}) copy-start(f32[2,2,2,128,128]{4,3,2,1,0:T(8,128)} %copy-done.6) | copy-start | bytes 1572868
  248.3 7.9 %copy-start.12 = (s32[16]{0:T(128)S(1)}, s32[16]{0:T(128)}, u32[]{:S(2)}) copy-start(s32[16]{0:T(128)} %param.13) | copy-start | bytes 196
  248.3 9.9 %collective-permute-start.3 = (f32[6,2,2,128,128]{4,3,2,1,0:T(8,128)S(1)}, f32[6,2,2,128,128]{4,3,2,1,0:T(8,128)S(1)}, u32[]{:S(2)}, u32[]{:S(2)}) collective-permute-start(f32[6,2,2,128,128]{4,3,2,1,0:T(8,128)S(1)} %shard_map.105.rest_0_), channel_id=1, source_target_pairs={{0,64},{64,0},{1,65},{65,1},{2,66},{66,2},{3,67},{67,3},{4,68},{68... | collective-permute-start | bytes 4718600 | tf_op jit(solution)/shard_map/ppermute | solution.py:264
  256.0 4.6 %collective-permute-start.2 = (f32[2,2,2,128,128]{4,3,2,1,0:T(8,128)S(1)}, f32[2,2,2,128,128]{4,3,2,1,0:T(8,128)S(1)}, u32[]{:S(2)}, u32[]{:S(2)}) collective-permute-start(f32[2,2,2,128,128]{4,3,2,1,0:T(8,128)S(1)} %shard_map.104.rest_1_), channel_id=1, source_target_pairs={{0,64},{64,0},{1,65},{65,1},{2,66},{66,2},{3,67},{67,3},{4,68},{68... | collective-permute-start | bytes 1572872 | tf_op jit(solution)/shard_map/ppermute | solution.py:264

commit v2 on v1

--- a/solution.py
+++ b/solution.py
@@ -46,12 +46,12 @@
     return high, (value - high.astype(F32)).astype(BF16)
 
 
-def collect_kernel(start, count, pool, local, *rest):
-    sent, own, done = rest[-3:]
-    half = local.shape[0] // 2
+def collect_kernel(parts, other, pool, local, *rest):
+    kept, done = rest[-1 - len(parts) : -1], rest[-1]
+    first = local.shape[0] // 2 * (1 - pool[0] if other else pool[0])
     copies = [
-        pltpu.make_async_copy(local.at[pl.ds(half * q + start, count)], kept, done.at[k])
-        for k, (q, kept) in enumerate(((1 - pool[0], sent), (pool[0], own)))
+        pltpu.make_async_copy(local.at[pl.ds(first + start, count)], part, done.at[k])
+        for k, ((start, count), part) in enumerate(zip(parts, kept))
     ]
     for copy in copies:
         copy.start()
@@ -172,8 +172,8 @@
     pool = lax.axis_index("pool").astype(jnp.int32).reshape(1)
     swap = [(0, 1), (1, 0)]
     limit = lambda share: pltpu.CompilerParams(vmem_limit_bytes=share << 20)
-    ahead = [(0, 2), (2, mine - 2)]
-    behind = ahead[::-1]
+    ahead = [(0, mine // 2), (mine // 2, mine // 2)]
+    behind = ahead
 
     forward = dft(n, -1.0)
     inverse = dft(n, 1.0)
@@ -189,20 +189,21 @@
     scalars = pl.BlockSpec(memory_space=pltpu.SMEM)
     parts = lambda count: jax.ShapeDtypeStruct((count, *tile), F32)
 
-    own, arrived, sends = [], [], []
-    for c, (start, count) in enumerate(ahead):
-        sent, kept = pl.pallas_call(
-            functools.partial(collect_kernel, start, count),
-            out_shape=(parts(count), parts(count)),
-            in_specs=[scalars, far] + [far] * c,
-            out_specs=(RESIDENT, RESIDENT),
-            scratch_shapes=[pltpu.SemaphoreType.DMA((2,))],
-            compiler_params=limit(52 if c == 0 else 49),
+    def collected(other, share):
+        return pl.pallas_call(
+            functools.partial(collect_kernel, ahead, other),
+            out_shape=tuple(parts(count) for _, count in ahead),
+            in_specs=[scalars, far],
+            out_specs=(RESIDENT,) * len(ahead),
+            scratch_shapes=[pltpu.SemaphoreType.DMA((len(ahead),))],
+            compiler_params=limit(share),
             cost_estimate=taking(1),
-        )(pool, local, *sends)
-        sends.append(sent)
-        own.append(kept)
+        )(pool, local)
+
+    arrived = []
+    for sent in collected(True, 49):
         arrived.append(lax.ppermute(sent, "pool", swap))
+    own = collected(False, 49)
 
     shape = (devices // 2, 2, planes, mine // 2, 8, n)
     spectrum = None

time: 262 us -> 258 us (0.985)
  waiting for transfers between devices: 100 us -> 94.7 us
    ppermute x2, waiting for transfers between devices: 3.64 us -> 0.47 us  [per_device(): arrived.append(lax.ppermute(sent, 'pool', swap))]
  transfers between devices with their start and end apart: 5 -> 5, of which waited for: 3 -> 3; matrix products, arithmetic and copies ran while one was open for 0% -> 0% of each run, Pallas kernels for 2% -> 3%
where the time goes in v2:
time: 258 us
  blocking collectives  104 us (40%)
  waiting for transfers between devices  94.7 us (37%)
  starting transfers between devices  37.5 us (15%)
  Pallas kernels  19.6 us (8%)
    all_to_all x1, blocking collectives, per_device(): lax.all_to_all(columns.reshape(flat), 'slab', split_axis=0, concat_axis=0...  104 us
    all_to_all x1, waiting for transfers between devices, per_device(): lax.all_to_all(spectrum.reshape(flat), 'slab', split_axis=0, concat_axis=...  94 us
    ppermute x2, starting transfers between devices, per_device(): arrived.append(lax.ppermute(sent, 'pool', swap))  20.7 us
    all_to_all x1, starting transfers between devices, per_device(): lax.all_to_all(spectrum.reshape(flat), 'slab', split_axis=0, concat_axis=...  9.77 us
    ppermute x2, starting transfers between devices, per_device(): others.append(lax.ppermute(results[-1], 'pool', swap))  6.99 us
    pallas_call x2, Pallas kernels, per_device(): pl.pallas_call(forward_kernel, out_shape=jax.ShapeDtypeStruct(shape, F32)...  5.22 us
  transfers between devices with their start and end apart: 5, of which 3 were waited for; matrix products, arithmetic and copies ran while one was open for 0% of the time, Pallas kernels for 3%

profile of v2, /device:TPU:33, one launch (start us, length us, event | category | flops | bytes accessed | tf_op | source)
XLA Modules:
  0.0 257.9 jit_solution(16296830453075212575)
XLA Ops:
  0.0 1.6 shard_map.101
  1.6 20.5 %collective-permute-start.1 = (f32[4,2,2,128,128]{4,3,2,1,0:T(8,128)S(1)}, f32[4,2,2,128,128]{4,3,2,1,0:T(8,128)S(1)}, u32[]{:S(2)}, u32[]{:S(2)}) collective-permute-start(f32[4,2,2,128,128]{4,3,2,1,0:T(8,128)S(1)} %get-tuple-element.12), channel_id=1, source_target_pairs={{0,64},{64,0},{1,65},{65,1},{2,66},{66,2},{3,67},{67,3},{4,68},{68... | collective-permute-start | bytes 3145736 | tf_op jit(solution)/shard_map/ppermute | solution.py:205
  22.1 0.2 collective-permute-start
  22.3 1.6 shard_map.100
  23.9 0.5 collective-permute-done.1.arrived
  24.4 2.6 %shard_map.102.rest_0_ = f32[32,2,2,4,8,128]{5,4,3,2,1,0:T(8,128)} custom-call(f32[4,2,2,128,128]{4,3,2,1,0:T(8,128)S(1)} %get-tuple-element.11.own, f32[4,2,2,128,128]{4,3,2,1,0:T(8,128)S(1)} %collective-permute-done.1.arrived, bf16[2,256,256]{2,1,0:T(8,128)(2,1)S(1)} %copy-done.6, bf16[2,2,256,256]{3,2,1,0:T(8,128)(2,1)S(1)} %copy-done.9), custom_call_target="tpu_custom_call" | custom-call | flops 240000000 | tf_op jit(solution)/shard_map/pallas_call | solution.py:218
  27.0 2.6 %shard_map.103 = f32[32,2,2,4,8,128]{5,4,3,2,1,0:T(8,128)} custom-call(f32[4,2,2,128,128]{4,3,2,1,0:T(8,128)S(1)} %get-tuple-element.9.own, f32[4,2,2,128,128]{4,3,2,1,0:T(8,128)S(1)} %collective-permute-done.arrived, bf16[2,256,256]{2,1,0:T(8,128)(2,1)S(1)} %copy-done.6, bf16[2,2,256,256]{3,2,1,0:T(8,128)(2,1)S(1)} %copy-done.9, ...), custom_call_target="tpu_custom_call", output_to_operand_aliasing={{}: (4, {})} | custom-call | flops 240000000 | tf_op jit(solution)/shard_map/pallas_call | solution.py:218
  29.6 9.8 %all-to-all-start = ((f32[64,64,128]{2,1,0:T(8,128)}), f32[64,64,128]{2,1,0:T(8,128)S(1)}, u32[]{:S(2)}, u32[]{:S(2)}) async-start(f32[64,64,128]{2,1,0:T(8,128)} %bitcast.2), calls=%async_computation | async-start | bytes 4194304 | tf_op jit(solution)/shard_map/all_to_all | solution.py:235
  39.5 0.1 broadcast_add_fusion
  39.5 1.0 fusion.kernel
  40.5 94.0 %all-to-all-done = f32[64,64,128]{2,1,0:T(8,128)S(1)} async-done(((f32[64,64,128]{2,1,0:T(8,128)}), f32[64,64,128]{2,1,0:T(8,128)S(1)}, u32[]{:S(2)}, u32[]{:S(2)}) %all-to-all-start) | async-done | bytes 2097184 | tf_op jit(solution)/shard_map/all_to_all | solution.py:235
  134.6 0.9 copy-done.7
  135.5 3.7 %middle.1 = f32[128,4,8,128]{3,2,1,0:T(8,128)S(1)} custom-call(f32[128,4,8,128]{3,2,1,0:T(8,128)S(1)} %bitcast.12, bf16[2,256,256]{2,1,0:T(8,128)(2,1)S(1)} %copy-done.7, bf16[2,256,256]{2,1,0:T(8,128)(2,1)S(1)} %copy-done.6, f32[2,128,128]{2,1,0:T(8,128)S(1)} %fusion.kernel), custom_call_target="tpu_custom_call" | custom-call | flops 400000000 | tf_op jit(solution)/shard_map/middle/pallas_call | solution.py:237
  139.3 0.0 copy-start.8
  139.3 0.0 copy-start.10
  139.3 103.7 %all_to_all.10 = f32[64,64,128]{2,1,0:T(8,128)S(1)} all-to-all(f32[64,64,128]{2,1,0:T(8,128)S(1)} %bitcast.13), channel_id=1, replica_groups=mesh['group'=2,'pool'=2,'slab'=64] {'slab'}, dimensions={0} | all-to-all | bytes 4194304 | tf_op jit(solution)/shard_map/all_to_all | solution.py:248
  243.1 1.8 shard_map.105.rest_0_
  244.9 6.8 %collective-permute-start.3 = (f32[4,2,2,128,128]{4,3,2,1,0:T(8,128)S(1)}, f32[4,2,2,128,128]{4,3,2,1,0:T(8,128)S(1)}, u32[]{:S(2)}, u32[]{:S(2)}) collective-permute-start(f32[4,2,2,128,128]{4,3,2,1,0:T(8,128)S(1)} %shard_map.105.rest_0_), channel_id=1, source_target_pairs={{0,64},{64,0},{1,65},{65,1},{2,66},{66,2},{3,67},{67,3},{4,68},{68... | collective-permute-start | bytes 3145736 | tf_op jit(solution)/shard_map/ppermute | solution.py:265
  251.7 1.8 shard_map.104.rest_1_
  253.5 0.2 collective-permute-start.2
  253.7 0.1 select_reduce_fusion.slot
  253.8 0.2 collective-permute-done.3.rest_2_
  254.0 2.3 shard_map.106.rest_1_
  256.3 1.5 shard_map.107
  (25 shorter events, 0.1 us)
Async XLA Ops:
  1.6 22.8 %collective-permute-start.1 = (f32[4,2,2,128,128]{4,3,2,1,0:T(8,128)S(1)}, f32[4,2,2,128,128]{4,3,2,1,0:T(8,128)S(1)}, u32[]{:S(2)}, u32[]{:S(2)}) collective-permute-start(f32[4,2,2,128,128]{4,3,2,1,0:T(8,128)S(1)} %get-tuple-element.12), channel_id=1, source_target_pairs={{0,64},{64,0},{1,65},{65,1},{2,66},{66,2},{3,67},{67,3},{4,68},{68... | collective-permute-start | bytes 3145736 | tf_op jit(solution)/shard_map/ppermute | solution.py:205
  22.1 2.3 copy-start.6
  22.1 2.3 copy-start.9
  22.1 4.9 %collective-permute-start = (f32[4,2,2,128,128]{4,3,2,1,0:T(8,128)S(1)}, f32[4,2,2,128,128]{4,3,2,1,0:T(8,128)S(1)}, u32[]{:S(2)}, u32[]{:S(2)}) collective-permute-start(f32[4,2,2,128,128]{4,3,2,1,0:T(8,128)S(1)} %get-tuple-element.10), channel_id=1, source_target_pairs={{0,64},{64,0},{1,65},{65,1},{2,66},{66,2},{3,67},{67,3},{4,68},{68... | collective-permute-start | bytes 3145736 | tf_op jit(solution)/shard_map/ppermute | solution.py:205
  23.9 3.1 %copy-start.4 = (f32[4,2,2,128,128]{4,3,2,1,0:T(8,128)}, f32[4,2,2,128,128]{4,3,2,1,0:T(8,128)S(1)}, u32[]{:S(2)}) copy-start(f32[4,2,2,128,128]{4,3,2,1,0:T(8,128)S(1)} %get-tuple-element.11.own) | copy-start | bytes 3145732
  23.9 3.1 %copy-start = (f32[4,2,2,128,128]{4,3,2,1,0:T(8,128)}, f32[4,2,2,128,128]{4,3,2,1,0:T(8,128)S(1)}, u32[]{:S(2)}) copy-start(f32[4,2,2,128,128]{4,3,2,1,0:T(8,128)S(1)} %get-tuple-element.9.own) | copy-start | bytes 3145732
  24.4 2.6 %copy-start.2 = (f32[4,2,2,128,128]{4,3,2,1,0:T(8,128)}, f32[4,2,2,128,128]{4,3,2,1,0:T(8,128)S(1)}, u32[]{:S(2)}) copy-start(f32[4,2,2,128,128]{4,3,2,1,0:T(8,128)S(1)} %collective-permute-done.1.arrived) | copy-start | bytes 3145732
  29.6 104.9 %all-to-all-start = ((f32[64,64,128]{2,1,0:T(8,128)}), f32[64,64,128]{2,1,0:T(8,128)S(1)}, u32[]{:S(2)}, u32[]{:S(2)}) async-start(f32[64,64,128]{2,1,0:T(8,128)} %bitcast.2), calls=%async_computation | async-start | bytes 4194304 | tf_op jit(solution)/shard_map/all_to_all | solution.py:235
  134.6 1.0 copy-start.7
  139.3 103.8 %copy-start.3 = (f32[4,2,2,128,128]{4,3,2,1,0:T(8,128)S(1)}, f32[4,2,2,128,128]{4,3,2,1,0:T(8,128)}, u32[]{:S(2)}) copy-start(f32[4,2,2,128,128]{4,3,2,1,0:T(8,128)} %copy-done.2) | copy-start | bytes 3145732
  139.3 103.8 %copy-start.5 = (f32[4,2,2,128,128]{4,3,2,1,0:T(8,128)S(1)}, f32[4,2,2,128,128]{4,3,2,1,0:T(8,128)}, u32[]{:S(2)}) copy-start(f32[4,2,2,128,128]{4,3,2,1,0:T(8,128)} %copy-done.4) | copy-start | bytes 3145732
  139.3 103.8 %copy-start.8 = (bf16[2,2,256,256]{3,2,1,0:T(8,128)(2,1)S(1)}, bf16[2,2,256,256]{3,2,1,0:T(8,128)(2,1)}, u32[]{:S(2)}) copy-start(bf16[2,2,256,256]{3,2,1,0:T(8,128)(2,1)} %constant.62.clone.wyi) | copy-start | bytes 1572868
  139.3 103.8 %copy-start.10 = (f32[2,128,128]{2,1,0:T(8,128)S(1)}, f32[2,128,128]{2,1,0:T(8,128)}, u32[]{:S(2)}) copy-start(f32[2,128,128]{2,1,0:T(8,128)} %fxc.3) | copy-start | bytes 393220
  243.1 8.7 %copy-start.1 = (f32[4,2,2,128,128]{4,3,2,1,0:T(8,128)S(1)}, f32[4,2,2,128,128]{4,3,2,1,0:T(8,128)}, u32[]{:S(2)}) copy-start(f32[4,2,2,128,128]{4,3,2,1,0:T(8,128)} %copy-done) | copy-start | bytes 3145732
  244.9 8.8 %copy-start.11 = (s32[16]{0:T(128)S(1)}, s32[16]{0:T(128)}, u32[]{:S(2)}) copy-start(s32[16]{0:T(128)} %param.13) | copy-start | bytes 196
  244.9 9.1 %collective-permute-start.3 = (f32[4,2,2,128,128]{4,3,2,1,0:T(8,128)S(1)}, f32[4,2,2,128,128]{4,3,2,1,0:T(8,128)S(1)}, u32[]{:S(2)}, u32[]{:S(2)}) collective-permute-start(f32[4,2,2,128,128]{4,3,2,1,0:T(8,128)S(1)} %shard_map.105.rest_0_), channel_id=1, source_target_pairs={{0,64},{64,0},{1,65},{65,1},{2,66},{66,2},{3,67},{67,3},{4,68},{68... | collective-permute-start | bytes 3145736 | tf_op jit(solution)/shard_map/ppermute | solution.py:265
  253.5 2.8 %collective-permute-start.2 = (f32[4,2,2,128,128]{4,3,2,1,0:T(8,128)S(1)}, f32[4,2,2,128,128]{4,3,2,1,0:T(8,128)S(1)}, u32[]{:S(2)}, u32[]{:S(2)}) collective-permute-start(f32[4,2,2,128,128]{4,3,2,1,0:T(8,128)S(1)} %shard_map.104.rest_1_), channel_id=1, source_target_pairs={{0,64},{64,0},{1,65},{65,1},{2,66},{66,2},{3,67},{67,3},{4,68},{68... | collective-permute-start | bytes 3145736 | tf_op jit(solution)/shard_map/ppermute | solution.py:265

commit v3 on v2

--- a/solution.py
+++ b/solution.py
@@ -27,6 +27,16 @@
     return np.block([[cosine, -sine], [sine, cosine]])
 
 
+def dft_halves(length, sign):
+    outputs = np.arange(length).reshape(-1, 2).T
+    parts = []
+    for k in outputs:
+        angle = 2.0 * np.pi * ((k[:, None] * np.arange(length // 2)[None, :]) % length) / length
+        cosine, sine = np.cos(angle), sign * np.sin(angle)
+        parts.append(np.block([[cosine, -sine], [sine, cosine]]))
+    return parts
+
+
 def dealt_rows(length, devices, swap):
     width = length // devices
     rows = []
@@ -46,9 +56,10 @@
     return high, (value - high.astype(F32)).astype(BF16)
 
 
-def collect_kernel(parts, other, pool, local, *rest):
+def collect_kernel(parts, other, local, *rest):
     kept, done = rest[-1 - len(parts) : -1], rest[-1]
-    first = local.shape[0] // 2 * (1 - pool[0] if other else pool[0])
+    pool = lax.axis_index("pool")
+    first = local.shape[0] // 2 * (1 - pool if other else pool)
     copies = [
         pltpu.make_async_copy(local.at[pl.ds(first + start, count)], part, done.at[k])
         for k, ((start, count), part) in enumerate(zip(parts, kept))
@@ -79,25 +90,44 @@
             spectrum[:, j, a, 0] = value[:, :, a * n : (a + 1) * n]
 
 
+def by_parts(table, even, odd):
+    dot = functools.partial(jnp.dot, preferred_element_type=F32)
+    (even_high, even_low), (odd_high, odd_low) = split(even), split(odd)
+    main = [
+        dot(jnp.concatenate([table[i, 0], table[i, 0]], axis=1), jnp.concatenate([high, low], axis=0))
+        for i, (high, low) in enumerate(((even_high, even_low), (odd_high, odd_low)))
+    ]
+    zero = jnp.zeros(table.shape[2:], BF16)
+    low = jnp.concatenate(
+        [jnp.concatenate([table[0, 1], zero], axis=1), jnp.concatenate([zero, table[1, 1]], axis=1)], axis=0
+    )
+    return jnp.concatenate(main, axis=0) + dot(low, jnp.concatenate([even_high, odd_high], axis=0))
+
+
 def middle_kernel(columns, wx, wxi, kernel, out, rows, back):
     n = kernel.shape[-1]
     length = kernel.shape[1]
+    half = length // 2
     step = pl.program_id(0)
     rows[...] = columns[:, step].reshape(rows.shape)
     grab = lambda j: rows[pl.ds(j, length, stride=8), :]
     order = [(p, b) for p in range(2) for b in range(2)]
-    real = jnp.concatenate([grab(4 * p + b) for p, b in order], axis=1)
-    imag = jnp.concatenate([grab(4 * p + 2 + b) for p, b in order], axis=1)
-    spectrum = dot3((wx[0], wx[1]), split(jnp.concatenate([real, imag], axis=0)))
-    both = jnp.concatenate([kernel[0], kernel[1]], axis=1)
-    both = jnp.concatenate([both, both], axis=1)
-    both = jnp.concatenate([both, both], axis=0)
-    result = dot3((wxi[0], wxi[1]), split(spectrum * both))
+    fields = [jnp.concatenate([grab(4 * p + 2 * r + b) for p, b in order], axis=1) for r in range(2)]
+    total = jnp.concatenate([f[:half] + f[half:] for f in fields], axis=0)
+    difference = jnp.concatenate([f[:half] - f[half:] for f in fields], axis=0)
+    spectrum = by_parts(wx, total, difference)
+    both = jnp.concatenate([kernel[0], kernel[1]] * 2, axis=1)
+    both = jnp.concatenate([both[:half], both[:half], both[half:], both[half:]], axis=0)
+    spectrum = spectrum * both
+    result = by_parts(wxi, spectrum[:length], spectrum[length:])
+    even, odd = result[:length], result[length:]
+    sides = (even + odd, even - odd)
     for i, (p, b) in enumerate(order):
         for r in range(2):
-            back[pl.ds(4 * p + 2 * r + b, length, stride=8), :] = result[
-                r * length : (r + 1) * length, i * n : (i + 1) * n
-            ]
+            for h, side in enumerate(sides):
+                back[pl.ds(h * half * 8 + 4 * p + 2 * r + b, half, stride=8), :] = side[
+                    r * half : (r + 1) * half, i * n : (i + 1) * n
+                ]
     out[:, step] = back[...].reshape(length, 8, n)
 
 
@@ -124,12 +154,13 @@
             out[2 * step + k, r] = part + fxc[...] * (own[2 * step + k, r] + arrived[2 * step + k, r])
 
 
-def place_kernel(pieces, slot, pool, *rest):
+def place_kernel(pieces, slot, *rest):
     parts, out, done = rest[: len(pieces)], rest[-2], rest[-1]
     half = out.shape[0] // 2
+    pool = lax.axis_index("pool")
     copies = []
     for (start, other), part in zip(pieces, parts):
-        first = half * (1 - pool[0] if other else pool[0]) + start
+        first = half * (1 - pool if other else pool) + start
         for k in range(part.shape[0]):
             copies.append(pltpu.make_async_copy(part.at[k], out.at[slot[first + k]], done.at[len(copies)]))
     for copy in copies:
@@ -146,12 +177,14 @@
     width = cutoff_mask.shape[1]
     start = lax.axis_index("slab") * width
     full_index = jnp.arange(length, dtype=jnp.int32)
+    dealt_index = full_index.reshape(-1, 2).T.reshape(-1)
     part_index = start + jnp.arange(width, dtype=jnp.int32)
-    full_square = frequency(full_index, length) ** 2
+    first_square = frequency(dealt_index, length) ** 2
     part_square = frequency(part_index, length) ** 2
-    total = part_square[:, None, None] + full_square[None, :, None] + full_square[None, None, :]
+    last_square = frequency(full_index, length) ** 2
+    total = part_square[:, None, None] + first_square[None, :, None] + last_square[None, None, :]
     unit = (2.0 * math.pi / length) ** 2
-    mask = jnp.swapaxes(cutoff_mask, 0, 1).astype(F32)
+    mask = cutoff_mask.reshape(-1, 2, width, length).transpose(2, 1, 0, 3).reshape(width, length, length).astype(F32)
     scale = 1.0 / float(length) ** 3
     return (4.0 * math.pi * mask / (unit * total + 0.25)) * scale
 
@@ -169,7 +202,6 @@
     devices = lax.axis_size("slab")
     mine = slots // 2
     tile = (2, planes, n, n)
-    pool = lax.axis_index("pool").astype(jnp.int32).reshape(1)
     swap = [(0, 1), (1, 0)]
     limit = lambda share: pltpu.CompilerParams(vmem_limit_bytes=share << 20)
     ahead = [(0, mine // 2), (mine // 2, mine // 2)]
@@ -182,8 +214,8 @@
     wzi = jnp.asarray(halves(inverse.T))
     wy = jnp.asarray(np.stack([halves(forward[rows]) for rows in dealt]))
     wyi = jnp.asarray(np.stack([halves(inverse[:, rows]) for rows in dealt]))
-    wx = jnp.asarray(halves(forward))
-    wxi = jnp.asarray(halves(inverse))
+    wx = jnp.asarray(np.stack([halves(w) for w in dft_halves(n, -1.0)]))
+    wxi = jnp.asarray(np.stack([halves(w.T) for w in dft_halves(n, -1.0)]))
 
     far = pl.BlockSpec(memory_space=pl.ANY)
     scalars = pl.BlockSpec(memory_space=pltpu.SMEM)
@@ -193,12 +225,12 @@
         return pl.pallas_call(
             functools.partial(collect_kernel, ahead, other),
             out_shape=tuple(parts(count) for _, count in ahead),
-            in_specs=[scalars, far],
+            in_specs=[far],
             out_specs=(RESIDENT,) * len(ahead),
             scratch_shapes=[pltpu.SemaphoreType.DMA((len(ahead),))],
             compiler_params=limit(share),
             cost_estimate=taking(1),
-        )(pool, local)
+        )(local)
 
     arrived = []
     for sent in collected(True, 49):
@@ -265,18 +297,18 @@
         others.append(lax.ppermute(results[-1], "pool", swap))
 
     def placed(pieces, arrays, out=None):
-        aliases = {} if out is None else {2 + len(arrays): 0}
+        aliases = {} if out is None else {1 + len(arrays): 0}
         kept = [] if out is None else [out]
         return pl.pallas_call(
             functools.partial(place_kernel, pieces),
             out_shape=jax.ShapeDtypeStruct(local.shape, F32),
-            in_specs=[scalars, scalars] + [RESIDENT] * len(arrays) + [far] * len(kept),
+            in_specs=[scalars] + [RESIDENT] * len(arrays) + [far] * len(kept),
             out_specs=far,
             scratch_shapes=[pltpu.SemaphoreType.DMA((sum(a.shape[0] for a in arrays),))],
             input_output_aliases=aliases,
             compiler_params=limit(40),
             cost_estimate=taking(1),
-        )(slot, pool, *arrays, *kept)
+        )(slot, *arrays, *kept)
 
     starts = [start for start, _ in behind]
     out = placed([(starts[0], False), (starts[1], False), (starts[0], True)], [*results, others[0]])

time: 258 us -> 257 us (level)
  transfers between devices with their start and end apart: 5 -> 5, of which waited for: 3 -> 3; matrix products, arithmetic and copies ran while one was open for 0% -> 1% of each run, Pallas kernels for 3% -> 3%
where the time goes in v3:
time: 257 us
  blocking collectives  104 us (40%)
  waiting for transfers between devices  93.9 us (37%)
  starting transfers between devices  37.6 us (15%)
  Pallas kernels  19.3 us (8%)
    all_to_all x1, blocking collectives, per_device(): lax.all_to_all(columns.reshape(flat), 'slab', split_axis=0, concat_axis=0...  104 us
    all_to_all x1, waiting for transfers between devices, per_device(): lax.all_to_all(spectrum.reshape(flat), 'slab', split_axis=0, concat_axis=...  93.2 us
    ppermute x2, starting transfers between devices, per_device(): arrived.append(lax.ppermute(sent, 'pool', swap))  20.7 us
    all_to_all x1, starting transfers between devices, per_device(): lax.all_to_all(spectrum.reshape(flat), 'slab', split_axis=0, concat_axis=...  9.9 us
    ppermute x2, starting transfers between devices, per_device(): others.append(lax.ppermute(results[-1], 'pool', swap))  6.98 us
    pallas_call x2, Pallas kernels, per_device(): pl.pallas_call(forward_kernel, out_shape=jax.ShapeDtypeStruct(shape, F32)...  5.22 us
  transfers between devices with their start and end apart: 5, of which 3 were waited for; matrix products, arithmetic and copies ran while one was open for 1% of the time, Pallas kernels for 3%

profile of v3, /device:TPU:33, one launch (start us, length us, event | category | flops | bytes accessed | tf_op | source)
XLA Modules:
  0.0 256.9 jit_solution(4358738305439837398)
XLA Ops:
  0.0 1.6 shard_map.101
  1.6 20.5 %collective-permute-start.1 = (f32[4,2,2,128,128]{4,3,2,1,0:T(8,128)S(1)}, f32[4,2,2,128,128]{4,3,2,1,0:T(8,128)S(1)}, u32[]{:S(2)}, u32[]{:S(2)}) collective-permute-start(f32[4,2,2,128,128]{4,3,2,1,0:T(8,128)S(1)} %get-tuple-element.12), channel_id=1, source_target_pairs={{0,64},{64,0},{1,65},{65,1},{2,66},{66,2},{3,67},{67,3},{4,68},{68... | collective-permute-start | bytes 3145736 | tf_op jit(solution)/shard_map/ppermute | solution.py:237
  22.1 0.2 collective-permute-start
  22.3 1.6 shard_map.100
  23.9 0.5 collective-permute-done.1.arrived
  24.4 2.6 %shard_map.102.rest_0_ = f32[32,2,2,4,8,128]{5,4,3,2,1,0:T(8,128)} custom-call(f32[4,2,2,128,128]{4,3,2,1,0:T(8,128)S(1)} %get-tuple-element.11.own, f32[4,2,2,128,128]{4,3,2,1,0:T(8,128)S(1)} %collective-permute-done.1.arrived, bf16[2,256,256]{2,1,0:T(8,128)(2,1)S(1)} %copy-done.8, bf16[2,2,256,256]{3,2,1,0:T(8,128)(2,1)S(1)} %copy-done.7), custom_call_target="tpu_custom_call" | custom-call | flops 240000000 | tf_op jit(solution)/shard_map/pallas_call | solution.py:250
  27.0 2.6 %shard_map.103 = f32[32,2,2,4,8,128]{5,4,3,2,1,0:T(8,128)} custom-call(f32[4,2,2,128,128]{4,3,2,1,0:T(8,128)S(1)} %get-tuple-element.9.own, f32[4,2,2,128,128]{4,3,2,1,0:T(8,128)S(1)} %collective-permute-done.arrived, bf16[2,256,256]{2,1,0:T(8,128)(2,1)S(1)} %copy-done.8, bf16[2,2,256,256]{3,2,1,0:T(8,128)(2,1)S(1)} %copy-done.7, ...), custom_call_target="tpu_custom_call", output_to_operand_aliasing={{}: (4, {})} | custom-call | flops 240000000 | tf_op jit(solution)/shard_map/pallas_call | solution.py:250
  29.6 9.9 %all-to-all-start = ((f32[64,64,128]{2,1,0:T(8,128)}), f32[64,64,128]{2,1,0:T(8,128)S(1)}, u32[]{:S(2)}, u32[]{:S(2)}) async-start(f32[64,64,128]{2,1,0:T(8,128)} %bitcast.1), calls=%async_computation | async-start | bytes 4194304 | tf_op jit(solution)/shard_map/all_to_all | solution.py:267
  39.6 0.1 add.128
  39.7 0.1 convert_multiply_fusion
  39.7 0.7 copy.14
  40.4 0.1 broadcast_add_fusion
  40.5 1.0 fusion.kernel
  41.5 93.2 %all-to-all-done = f32[64,64,128]{2,1,0:T(8,128)S(1)} async-done(((f32[64,64,128]{2,1,0:T(8,128)}), f32[64,64,128]{2,1,0:T(8,128)S(1)}, u32[]{:S(2)}, u32[]{:S(2)}) %all-to-all-start) | async-done | bytes 2097184 | tf_op jit(solution)/shard_map/all_to_all | solution.py:267
  134.7 3.4 %middle.1 = f32[128,4,8,128]{3,2,1,0:T(8,128)S(1)} custom-call(f32[128,4,8,128]{3,2,1,0:T(8,128)S(1)} %bitcast.14, bf16[2,2,128,128]{3,2,1,0:T(8,128)(2,1)S(1)} %copy-done.12, bf16[2,2,128,128]{3,2,1,0:T(8,128)(2,1)S(1)} %copy-done.11, f32[2,128,128]{2,1,0:T(8,128)S(1)} %fusion.kernel), custom_call_target="tpu_custom_call" | custom-call | flops 400000000 | tf_op jit(solution)/shard_map/middle/pallas_call | solution.py:269
  138.2 103.9 %all_to_all.10 = f32[64,64,128]{2,1,0:T(8,128)S(1)} all-to-all(f32[64,64,128]{2,1,0:T(8,128)S(1)} %bitcast.15), channel_id=1, replica_groups=mesh['group'=2,'pool'=2,'slab'=64] {'slab'}, dimensions={0} | all-to-all | bytes 4194304 | tf_op jit(solution)/shard_map/all_to_all | solution.py:280
  242.1 1.8 shard_map.105.rest_0_
  243.9 6.8 %collective-permute-start.3 = (f32[4,2,2,128,128]{4,3,2,1,0:T(8,128)S(1)}, f32[4,2,2,128,128]{4,3,2,1,0:T(8,128)S(1)}, u32[]{:S(2)}, u32[]{:S(2)}) collective-permute-start(f32[4,2,2,128,128]{4,3,2,1,0:T(8,128)S(1)} %shard_map.105.rest_0_), channel_id=1, source_target_pairs={{0,64},{64,0},{1,65},{65,1},{2,66},{66,2},{3,67},{67,3},{4,68},{68... | collective-permute-start | bytes 3145736 | tf_op jit(solution)/shard_map/ppermute | solution.py:297
  250.7 1.8 shard_map.104.rest_1_
  252.5 0.2 collective-permute-start.2
  252.7 0.1 select_reduce_fusion.slot
  252.8 0.2 collective-permute-done.3.rest_2_
  253.0 2.3 shard_map.106.rest_1_
  255.3 1.6 shard_map.107
  (36 shorter events, 0.1 us)
Async XLA Ops:
  1.6 22.8 %collective-permute-start.1 = (f32[4,2,2,128,128]{4,3,2,1,0:T(8,128)S(1)}, f32[4,2,2,128,128]{4,3,2,1,0:T(8,128)S(1)}, u32[]{:S(2)}, u32[]{:S(2)}) collective-permute-start(f32[4,2,2,128,128]{4,3,2,1,0:T(8,128)S(1)} %get-tuple-element.12), channel_id=1, source_target_pairs={{0,64},{64,0},{1,65},{65,1},{2,66},{66,2},{3,67},{67,3},{4,68},{68... | collective-permute-start | bytes 3145736 | tf_op jit(solution)/shard_map/ppermute | solution.py:237
  22.1 2.3 copy-start.7
  22.1 2.3 copy-start.8
  22.1 4.9 %collective-permute-start = (f32[4,2,2,128,128]{4,3,2,1,0:T(8,128)S(1)}, f32[4,2,2,128,128]{4,3,2,1,0:T(8,128)S(1)}, u32[]{:S(2)}, u32[]{:S(2)}) collective-permute-start(f32[4,2,2,128,128]{4,3,2,1,0:T(8,128)S(1)} %get-tuple-element.10), channel_id=1, source_target_pairs={{0,64},{64,0},{1,65},{65,1},{2,66},{66,2},{3,67},{67,3},{4,68},{68... | collective-permute-start | bytes 3145736 | tf_op jit(solution)/shard_map/ppermute | solution.py:237
  23.9 3.1 %copy-start.4 = (f32[4,2,2,128,128]{4,3,2,1,0:T(8,128)}, f32[4,2,2,128,128]{4,3,2,1,0:T(8,128)S(1)}, u32[]{:S(2)}) copy-start(f32[4,2,2,128,128]{4,3,2,1,0:T(8,128)S(1)} %get-tuple-element.11.own) | copy-start | bytes 3145732
  23.9 3.1 %copy-start = (f32[4,2,2,128,128]{4,3,2,1,0:T(8,128)}, f32[4,2,2,128,128]{4,3,2,1,0:T(8,128)S(1)}, u32[]{:S(2)}) copy-start(f32[4,2,2,128,128]{4,3,2,1,0:T(8,128)S(1)} %get-tuple-element.9.own) | copy-start | bytes 3145732
  24.4 2.6 %copy-start.2 = (f32[4,2,2,128,128]{4,3,2,1,0:T(8,128)}, f32[4,2,2,128,128]{4,3,2,1,0:T(8,128)S(1)}, u32[]{:S(2)}) copy-start(f32[4,2,2,128,128]{4,3,2,1,0:T(8,128)S(1)} %collective-permute-done.1.arrived) | copy-start | bytes 3145732
  29.6 10.0 %copy-start.13 = (s32[128,2,128]{2,1,0:T(2,128)S(1)}, s32[128,2,128]{2,1,0:T(2,128)}, u32[]{:S(2)}) copy-start(s32[128,2,128]{2,1,0:T(2,128)} %param.12) | copy-start | bytes 393220
  29.6 105.1 %copy-start.11 = (bf16[2,2,128,128]{3,2,1,0:T(8,128)(2,1)S(1)}, bf16[2,2,128,128]{3,2,1,0:T(8,128)(2,1)}, u32[]{:S(2)}) copy-start(bf16[2,2,128,128]{3,2,1,0:T(8,128)(2,1)} %constant.68.clone.wxi) | copy-start | bytes 393220
  29.6 105.1 %copy-start.12 = (bf16[2,2,128,128]{3,2,1,0:T(8,128)(2,1)S(1)}, bf16[2,2,128,128]{3,2,1,0:T(8,128)(2,1)}, u32[]{:S(2)}) copy-start(bf16[2,2,128,128]{3,2,1,0:T(8,128)(2,1)} %constant.67.clone.wx) | copy-start | bytes 393220
  29.6 105.1 %all-to-all-start = ((f32[64,64,128]{2,1,0:T(8,128)}), f32[64,64,128]{2,1,0:T(8,128)S(1)}, u32[]{:S(2)}, u32[]{:S(2)}) async-start(f32[64,64,128]{2,1,0:T(8,128)} %bitcast.1), calls=%async_computation | async-start | bytes 4194304 | tf_op jit(solution)/shard_map/all_to_all | solution.py:267
  138.1 103.9 %copy-start.3 = (f32[4,2,2,128,128]{4,3,2,1,0:T(8,128)S(1)}, f32[4,2,2,128,128]{4,3,2,1,0:T(8,128)}, u32[]{:S(2)}) copy-start(f32[4,2,2,128,128]{4,3,2,1,0:T(8,128)} %copy-done.2) | copy-start | bytes 3145732
  138.1 103.9 %copy-start.5 = (f32[4,2,2,128,128]{4,3,2,1,0:T(8,128)S(1)}, f32[4,2,2,128,128]{4,3,2,1,0:T(8,128)}, u32[]{:S(2)}) copy-start(f32[4,2,2,128,128]{4,3,2,1,0:T(8,128)} %copy-done.4) | copy-start | bytes 3145732
  138.1 103.9 %copy-start.6 = (bf16[2,2,256,256]{3,2,1,0:T(8,128)(2,1)S(1)}, bf16[2,2,256,256]{3,2,1,0:T(8,128)(2,1)}, u32[]{:S(2)}) copy-start(bf16[2,2,256,256]{3,2,1,0:T(8,128)(2,1)} %constant.66.clone.wyi) | copy-start | bytes 1572868
  138.2 103.9 %copy-start.9 = (bf16[2,256,256]{2,1,0:T(8,128)(2,1)S(1)}, bf16[2,256,256]{2,1,0:T(8,128)(2,1)}, u32[]{:S(2)}) copy-start(bf16[2,256,256]{2,1,0:T(8,128)(2,1)} %constant.64.clone.wzi) | copy-start | bytes 786436
  138.2 103.9 %copy-start.10 = (f32[2,128,128]{2,1,0:T(8,128)S(1)}, f32[2,128,128]{2,1,0:T(8,128)}, u32[]{:S(2)}) copy-start(f32[2,128,128]{2,1,0:T(8,128)} %fxc.3) | copy-start | bytes 393220
  242.1 8.7 %copy-start.1 = (f32[4,2,2,128,128]{4,3,2,1,0:T(8,128)S(1)}, f32[4,2,2,128,128]{4,3,2,1,0:T(8,128)}, u32[]{:S(2)}) copy-start(f32[4,2,2,128,128]{4,3,2,1,0:T(8,128)} %copy-done) | copy-start | bytes 3145732
  243.9 8.8 %copy-start.14 = (s32[16]{0:T(128)S(1)}, s32[16]{0:T(128)}, u32[]{:S(2)}) copy-start(s32[16]{0:T(128)} %param.13) | copy-start | bytes 196
  243.9 9.1 %collective-permute-start.3 = (f32[4,2,2,128,128]{4,3,2,1,0:T(8,128)S(1)}, f32[4,2,2,128,128]{4,3,2,1,0:T(8,128)S(1)}, u32[]{:S(2)}, u32[]{:S(2)}) collective-permute-start(f32[4,2,2,128,128]{4,3,2,1,0:T(8,128)S(1)} %shard_map.105.rest_0_), channel_id=1, source_target_pairs={{0,64},{64,0},{1,65},{65,1},{2,66},{66,2},{3,67},{67,3},{4,68},{68... | collective-permute-start | bytes 3145736 | tf_op jit(solution)/shard_map/ppermute | solution.py:297
  252.5 2.8 %collective-permute-start.2 = (f32[4,2,2,128,128]{4,3,2,1,0:T(8,128)S(1)}, f32[4,2,2,128,128]{4,3,2,1,0:T(8,128)S(1)}, u32[]{:S(2)}, u32[]{:S(2)}) collective-permute-start(f32[4,2,2,128,128]{4,3,2,1,0:T(8,128)S(1)} %shard_map.104.rest_1_), channel_id=1, source_target_pairs={{0,64},{64,0},{1,65},{65,1},{2,66},{66,2},{3,67},{67,3},{4,68},{68... | collective-permute-start | bytes 3145736 | tf_op jit(solution)/shard_map/ppermute | solution.py:297

commit v4 on v3

--- a/solution.py
+++ b/solution.py
@@ -46,9 +46,20 @@
     return np.array(rows)
 
 
-def dot3(left, right):
+def table_first(table, value):
     dot = functools.partial(jnp.dot, preferred_element_type=F32)
-    return dot(left[0], right[0]) + (dot(left[0], right[1]) + dot(left[1], right[0]))
+    high, low = split(value)
+    m = table.shape[1]
+    both = dot(jnp.concatenate([table[0], table[1]], axis=0), high)
+    return both[:m] + (both[m:] + dot(table[0], low))
+
+
+def table_last(value, table):
+    dot = functools.partial(jnp.dot, preferred_element_type=F32)
+    high, low = split(value)
+    m = value.shape[0]
+    both = dot(jnp.concatenate([high, low], axis=0), table[0])
+    return both[:m] + (both[m:] + dot(high, table[1]))
 
 
 def split(value):
@@ -70,24 +81,61 @@
         copy.wait()
 
 
-def forward_kernel(own, arrived, wz, wy, *rest):
-    spectrum = rest[-1]
+def transformed(x, wz, wy):
+    n = x.shape[-1]
+    rows = jnp.concatenate([x[:, 0].reshape(4 * n, n), x[:, 1].reshape(4 * n, n)], axis=1)
+    y = table_last(rows, wz)
+    mixed = []
+    for k in range(2):
+        first, second = y[2 * k * n : (2 * k + 1) * n], y[(2 * k + 1) * n : (2 * k + 2) * n]
+        real = jnp.concatenate([first[:, :n], second[:, :n]], axis=1)
+        imag = jnp.concatenate([first[:, n:], second[:, n:]], axis=1)
+        mixed.append(table_first(wy[k], jnp.concatenate([real, imag], axis=0)).reshape(-1, 8, 2 * n))
+    even, odd = mixed
+    lower = lax.broadcasted_iota(jnp.int32, even.shape, 1) < 4
+    return jnp.where(lower, even, odd), jnp.where(lower, odd, even)
+
+
+def forward_first_kernel(own, arrived, wz, wy, tiles):
     n = own.shape[-1]
     step = pl.program_id(0)
-    mixed = []
-    for k in range(2):
-        x = own[2 * step + k] + arrived[2 * step + k]
-        rows = jnp.concatenate([x[0].reshape(2 * n, n), x[1].reshape(2 * n, n)], axis=1)
-        y = dot3(split(rows), (wz[0], wz[1]))
-        real = jnp.concatenate([y[:n, :n], y[n:, :n]], axis=1)
-        imag = jnp.concatenate([y[:n, n:], y[n:, n:]], axis=1)
-        stacked = split(jnp.concatenate([real, imag], axis=0))
-        mixed.append(dot3((wy[k, 0], wy[k, 1]), stacked).reshape(-1, 8, 2 * n))
-    even, odd = mixed
-    lower = lax.broadcasted_iota(jnp.int32, even.shape, 1) < 4
-    for j, value in enumerate((jnp.where(lower, even, odd), jnp.where(lower, odd, even))):
+    pair = pl.ds(2 * step, 2)
+    for j, value in enumerate(transformed(own[pair] + arrived[pair], wz[...], wy[...])):
         for a in range(2):
-            spectrum[:, j, a, 0] = value[:, :, a * n : (a + 1) * n]
+            tiles[:, j, a, step] = value[:, :, a * n : (a + 1) * n]
+
+
+def forward_second_kernel(own, arrived, wz, wy, tiles, spectrum, later, done):
+    n = own.shape[-1]
+    step = pl.program_id(0)
+    last = pl.num_programs(0) - 1
+    ready = tiles.shape[3]
+    earlier = pltpu.make_async_copy(tiles, spectrum.at[:, :, :, pl.ds(0, ready)], done.at[0])
+
+    @pl.when(step == 0)
+    def _():
+        earlier.start()
+
+    pair = pl.ds(2 * step, 2)
+    for j, value in enumerate(transformed(own[pair] + arrived[pair], wz[...], wy[...])):
+        for a in range(2):
+            later[step, :, j, a] = value[:, :, a * n : (a + 1) * n]
+
+    sent = [
+        pltpu.make_async_copy(later.at[i], spectrum.at[:, :, :, ready + i], done.at[1 + i])
+        for i in range(spectrum.shape[3] - ready)
+    ]
+    for i, copy in enumerate(sent):
+
+        @pl.when(step == i)
+        def _(copy=copy):
+            copy.start()
+
+    @pl.when(step == last)
+    def _():
+        earlier.wait()
+        for copy in sent:
+            copy.wait()
 
 
 def by_parts(table, even, odd):
@@ -139,18 +187,15 @@
     lower = lax.broadcasted_iota(jnp.int32, tiles[0].shape, 1) < 4
     even = jnp.where(lower, tiles[0], tiles[1])
     odd = jnp.where(lower, tiles[1], tiles[0])
+    rows = []
     for k, value in enumerate((even, odd)):
-        y = dot3((wyi[k, 0], wyi[k, 1]), split(value.reshape(2 * n, 2 * n)))
-        rows = jnp.concatenate(
-            [
-                jnp.concatenate([y[:n, a * n : (a + 1) * n], y[n:, a * n : (a + 1) * n]], axis=1)
-                for a in range(2)
-            ],
-            axis=0,
-        )
-        x = dot3(split(rows), (wzi[0], wzi[1]))
+        y = table_first(wyi[k], value.reshape(2 * n, 2 * n))
+        for a in range(2):
+            rows.append(jnp.concatenate([y[:n, a * n : (a + 1) * n], y[n:, a * n : (a + 1) * n]], axis=1))
+    x = table_last(jnp.concatenate(rows, axis=0), wzi[...])
+    for k in range(2):
         for r in range(2):
-            part = x[:, r * n : (r + 1) * n].reshape(2, n, n)
+            part = x[2 * k * n : (2 * k + 2) * n, r * n : (r + 1) * n].reshape(2, n, n)
             out[2 * step + k, r] = part + fxc[...] * (own[2 * step + k, r] + arrived[2 * step + k, r])
 
 
@@ -238,27 +283,32 @@
     own = collected(False, 49)
 
     shape = (devices // 2, 2, planes, mine // 2, 8, n)
-    spectrum = None
-    for c, (start, count) in enumerate(ahead):
-        operands = [own[c], arrived[c], wz, wy]
-        specs = [RESIDENT] * 4
-        aliases = {}
-        if spectrum is not None:
-            aliases = {len(operands): 0}
-            operands.append(spectrum)
-            specs.append(far)
-        spectrum = pl.pallas_call(
-            forward_kernel,
-            out_shape=jax.ShapeDtypeStruct(shape, F32),
-            grid=(count // 2,),
-            in_specs=specs,
-            out_specs=pl.BlockSpec(
-                (devices // 2, 2, planes, 1, 8, n), lambda i, start=start: (0, 0, 0, start // 2 + i, 0, 0)
-            ),
-            input_output_aliases=aliases,
-            compiler_params=limit(40),
-            cost_estimate=taking(0.6 * count),
-        )(*operands)
+    ready = ahead[0][1] // 2
+    tiles = pl.pallas_call(
+        forward_first_kernel,
+        out_shape=jax.ShapeDtypeStruct((*shape[:3], ready, *shape[4:]), F32),
+        grid=(ready,),
+        in_specs=[RESIDENT] * 4,
+        out_specs=RESIDENT,
+        compiler_params=limit(40),
+        cost_estimate=taking(2.4),
+        name="forward0",
+    )(own[0], arrived[0], wz, wy)
+    later = shape[3] - ready
+    spectrum = pl.pallas_call(
+        forward_second_kernel,
+        out_shape=jax.ShapeDtypeStruct(shape, F32),
+        grid=(later,),
+        in_specs=[RESIDENT] * 5,
+        out_specs=far,
+        scratch_shapes=[
+            pltpu.VMEM((later, *shape[:3], *shape[4:]), F32),
+            pltpu.SemaphoreType.DMA((1 + later,)),
+        ],
+        compiler_params=limit(40),
+        cost_estimate=taking(2.4),
+        name="forward1",
+    )(own[1], arrived[1], wz, wy, tiles)
 
     kernel = column_kernel(cutoff_mask, n)
     index = jnp.arange(slots, dtype=jnp.int32)

time: 257 us -> 257 us (level)
  no operation moved by 1% of the time
where the time goes in v4:
time: 257 us; the launch traced here: 256 us
  blocking collectives  104 us (40%)
  waiting for transfers between devices  94.2 us (37%)
  starting transfers between devices  37.6 us (15%)
  Pallas kernels  18.3 us (7%)
    all_to_all x1, blocking collectives, per_device(): lax.all_to_all(columns.reshape(flat), 'slab', split_axis=0, concat_axis=0...  104 us
    all_to_all x1, waiting for transfers between devices, per_device(): lax.all_to_all(spectrum.reshape(flat), 'slab', split_axis=0, concat_axis=...  93.2 us
    ppermute x2, starting transfers between devices, per_device(): arrived.append(lax.ppermute(sent, 'pool', swap))  20.7 us
    all_to_all x1, starting transfers between devices, per_device(): lax.all_to_all(spectrum.reshape(flat), 'slab', split_axis=0, concat_axis=...  9.92 us
    ppermute x2, starting transfers between devices, per_device(): others.append(lax.ppermute(results[-1], 'pool', swap))  6.98 us
  transfers between devices with their start and end apart: 5, of which 3 were waited for; matrix products, arithmetic and copies ran while one was open for 1% of the time, Pallas kernels for 3%

profile of v4, /device:TPU:33, one launch (start us, length us, event | category | flops | bytes accessed | tf_op | source)
XLA Modules:
  0.0 256.4 jit_solution(1800614343089772353)
XLA Ops:
  0.0 1.6 shard_map.101
  1.6 20.5 %collective-permute-start.1 = (f32[4,2,2,128,128]{4,3,2,1,0:T(8,128)S(1)}, f32[4,2,2,128,128]{4,3,2,1,0:T(8,128)S(1)}, u32[]{:S(2)}, u32[]{:S(2)}) collective-permute-start(f32[4,2,2,128,128]{4,3,2,1,0:T(8,128)S(1)} %get-tuple-element.12), channel_id=1, source_target_pairs={{0,64},{64,0},{1,65},{65,1},{2,66},{66,2},{3,67},{67,3},{4,68},{68... | collective-permute-start | bytes 3145736 | tf_op jit(solution)/shard_map/ppermute | solution.py:282
  22.1 0.2 collective-permute-start
  22.3 1.6 shard_map.100
  23.9 0.5 collective-permute-done.1.arrived
  24.4 2.1 forward0.1.tiles
  26.5 2.9 %forward1.1 = f32[32,2,2,4,8,128]{5,4,3,2,1,0:T(8,128)} custom-call(f32[4,2,2,128,128]{4,3,2,1,0:T(8,128)S(1)} %get-tuple-element.9.own, f32[4,2,2,128,128]{4,3,2,1,0:T(8,128)S(1)} %collective-permute-done.arrived, bf16[2,256,256]{2,1,0:T(8,128)(2,1)S(1)} %copy-done.9, bf16[2,2,256,256]{3,2,1,0:T(8,128)(2,1)S(1)} %copy-done.7, ...), custom_call_target="tpu_custom_call" | custom-call | flops 240000000 | tf_op jit(solution)/shard_map/forward1/pallas_call | solution.py:298
  29.4 9.9 %all-to-all-start = ((f32[64,64,128]{2,1,0:T(8,128)}), f32[64,64,128]{2,1,0:T(8,128)S(1)}, u32[]{:S(2)}, u32[]{:S(2)}) async-start(f32[64,64,128]{2,1,0:T(8,128)} %bitcast.1), calls=%async_computation | async-start | bytes 4194304 | tf_op jit(solution)/shard_map/all_to_all | solution.py:317
  39.4 0.1 add.128
  39.5 0.1 convert_multiply_fusion
  39.5 0.7 copy.13
  40.2 0.1 broadcast_add_fusion
  40.3 1.0 fusion.kernel
  41.3 93.2 %all-to-all-done = f32[64,64,128]{2,1,0:T(8,128)S(1)} async-done(((f32[64,64,128]{2,1,0:T(8,128)}), f32[64,64,128]{2,1,0:T(8,128)S(1)}, u32[]{:S(2)}, u32[]{:S(2)}) %all-to-all-start) | async-done | bytes 2097184 | tf_op jit(solution)/shard_map/all_to_all | solution.py:317
  134.5 3.4 %middle.1 = f32[128,4,8,128]{3,2,1,0:T(8,128)S(1)} custom-call(f32[128,4,8,128]{3,2,1,0:T(8,128)S(1)} %bitcast.14, bf16[2,2,128,128]{3,2,1,0:T(8,128)(2,1)S(1)} %copy-done.12, bf16[2,2,128,128]{3,2,1,0:T(8,128)(2,1)S(1)} %copy-done.11, f32[2,128,128]{2,1,0:T(8,128)S(1)} %fusion.kernel), custom_call_target="tpu_custom_call" | custom-call | flops 400000000 | tf_op jit(solution)/shard_map/middle/pallas_call | solution.py:319
  138.0 103.9 %all_to_all.10 = f32[64,64,128]{2,1,0:T(8,128)S(1)} all-to-all(f32[64,64,128]{2,1,0:T(8,128)S(1)} %bitcast.15), channel_id=1, replica_groups=mesh['group'=2,'pool'=2,'slab'=64] {'slab'}, dimensions={0} | all-to-all | bytes 4194304 | tf_op jit(solution)/shard_map/all_to_all | solution.py:330
  241.9 1.5 shard_map.103.rest_0_
  243.4 6.8 %collective-permute-start.3 = (f32[4,2,2,128,128]{4,3,2,1,0:T(8,128)S(1)}, f32[4,2,2,128,128]{4,3,2,1,0:T(8,128)S(1)}, u32[]{:S(2)}, u32[]{:S(2)}) collective-permute-start(f32[4,2,2,128,128]{4,3,2,1,0:T(8,128)S(1)} %shard_map.103.rest_0_), channel_id=1, source_target_pairs={{0,64},{64,0},{1,65},{65,1},{2,66},{66,2},{3,67},{67,3},{4,68},{68... | collective-permute-start | bytes 3145736 | tf_op jit(solution)/shard_map/ppermute | solution.py:347
  250.2 1.5 shard_map.102.rest_1_
  251.7 0.2 collective-permute-start.2
  251.8 0.1 select_reduce_fusion.slot
  252.0 0.5 collective-permute-done.3.rest_2_
  252.5 2.3 shard_map.104.rest_1_
  254.8 1.6 shard_map.105
  (36 shorter events, 0.1 us)
Async XLA Ops:
  1.6 22.8 %collective-permute-start.1 = (f32[4,2,2,128,128]{4,3,2,1,0:T(8,128)S(1)}, f32[4,2,2,128,128]{4,3,2,1,0:T(8,128)S(1)}, u32[]{:S(2)}, u32[]{:S(2)}) collective-permute-start(f32[4,2,2,128,128]{4,3,2,1,0:T(8,128)S(1)} %get-tuple-element.12), channel_id=1, source_target_pairs={{0,64},{64,0},{1,65},{65,1},{2,66},{66,2},{3,67},{67,3},{4,68},{68... | collective-permute-start | bytes 3145736 | tf_op jit(solution)/shard_map/ppermute | solution.py:282
  22.1 2.3 copy-start.7
  22.1 2.3 copy-start.9
  22.1 4.4 %collective-permute-start = (f32[4,2,2,128,128]{4,3,2,1,0:T(8,128)S(1)}, f32[4,2,2,128,128]{4,3,2,1,0:T(8,128)S(1)}, u32[]{:S(2)}, u32[]{:S(2)}) collective-permute-start(f32[4,2,2,128,128]{4,3,2,1,0:T(8,128)S(1)} %get-tuple-element.10), channel_id=1, source_target_pairs={{0,64},{64,0},{1,65},{65,1},{2,66},{66,2},{3,67},{67,3},{4,68},{68... | collective-permute-start | bytes 3145736 | tf_op jit(solution)/shard_map/ppermute | solution.py:282
  23.9 5.5 %copy-start = (f32[4,2,2,128,128]{4,3,2,1,0:T(8,128)}, f32[4,2,2,128,128]{4,3,2,1,0:T(8,128)S(1)}, u32[]{:S(2)}) copy-start(f32[4,2,2,128,128]{4,3,2,1,0:T(8,128)S(1)} %get-tuple-element.9.own) | copy-start | bytes 3145732
  23.9 5.5 %copy-start.4 = (f32[4,2,2,128,128]{4,3,2,1,0:T(8,128)}, f32[4,2,2,128,128]{4,3,2,1,0:T(8,128)S(1)}, u32[]{:S(2)}) copy-start(f32[4,2,2,128,128]{4,3,2,1,0:T(8,128)S(1)} %get-tuple-element.11.own) | copy-start | bytes 3145732
  24.4 5.0 %copy-start.2 = (f32[4,2,2,128,128]{4,3,2,1,0:T(8,128)}, f32[4,2,2,128,128]{4,3,2,1,0:T(8,128)S(1)}, u32[]{:S(2)}) copy-start(f32[4,2,2,128,128]{4,3,2,1,0:T(8,128)S(1)} %collective-permute-done.1.arrived) | copy-start | bytes 3145732
  29.4 10.1 %copy-start.13 = (s32[128,2,128]{2,1,0:T(2,128)S(1)}, s32[128,2,128]{2,1,0:T(2,128)}, u32[]{:S(2)}) copy-start(s32[128,2,128]{2,1,0:T(2,128)} %param.12) | copy-start | bytes 393220
  29.4 105.1 %copy-start.11 = (bf16[2,2,128,128]{3,2,1,0:T(8,128)(2,1)S(1)}, bf16[2,2,128,128]{3,2,1,0:T(8,128)(2,1)}, u32[]{:S(2)}) copy-start(bf16[2,2,128,128]{3,2,1,0:T(8,128)(2,1)} %constant.68.clone.wxi) | copy-start | bytes 393220
  29.4 105.1 %copy-start.12 = (bf16[2,2,128,128]{3,2,1,0:T(8,128)(2,1)S(1)}, bf16[2,2,128,128]{3,2,1,0:T(8,128)(2,1)}, u32[]{:S(2)}) copy-start(bf16[2,2,128,128]{3,2,1,0:T(8,128)(2,1)} %constant.67.clone.wx) | copy-start | bytes 393220
  29.4 105.1 %all-to-all-start = ((f32[64,64,128]{2,1,0:T(8,128)}), f32[64,64,128]{2,1,0:T(8,128)S(1)}, u32[]{:S(2)}, u32[]{:S(2)}) async-start(f32[64,64,128]{2,1,0:T(8,128)} %bitcast.1), calls=%async_computation | async-start | bytes 4194304 | tf_op jit(solution)/shard_map/all_to_all | solution.py:317
  137.9 104.0 %copy-start.3 = (f32[4,2,2,128,128]{4,3,2,1,0:T(8,128)S(1)}, f32[4,2,2,128,128]{4,3,2,1,0:T(8,128)}, u32[]{:S(2)}) copy-start(f32[4,2,2,128,128]{4,3,2,1,0:T(8,128)} %copy-done.2) | copy-start | bytes 3145732
  137.9 103.9 %copy-start.5 = (f32[4,2,2,128,128]{4,3,2,1,0:T(8,128)S(1)}, f32[4,2,2,128,128]{4,3,2,1,0:T(8,128)}, u32[]{:S(2)}) copy-start(f32[4,2,2,128,128]{4,3,2,1,0:T(8,128)} %copy-done.4) | copy-start | bytes 3145732
  137.9 103.9 %copy-start.6 = (bf16[2,2,256,256]{3,2,1,0:T(8,128)(2,1)S(1)}, bf16[2,2,256,256]{3,2,1,0:T(8,128)(2,1)}, u32[]{:S(2)}) copy-start(bf16[2,2,256,256]{3,2,1,0:T(8,128)(2,1)} %constant.66.clone.wyi) | copy-start | bytes 1572868
  137.9 103.9 %copy-start.8 = (bf16[2,256,256]{2,1,0:T(8,128)(2,1)S(1)}, bf16[2,256,256]{2,1,0:T(8,128)(2,1)}, u32[]{:S(2)}) copy-start(bf16[2,256,256]{2,1,0:T(8,128)(2,1)} %constant.64.clone.wzi) | copy-start | bytes 786436
  138.0 103.9 %copy-start.10 = (f32[2,128,128]{2,1,0:T(8,128)S(1)}, f32[2,128,128]{2,1,0:T(8,128)}, u32[]{:S(2)}) copy-start(f32[2,128,128]{2,1,0:T(8,128)} %fxc.3) | copy-start | bytes 393220
  241.9 8.3 %copy-start.1 = (f32[4,2,2,128,128]{4,3,2,1,0:T(8,128)S(1)}, f32[4,2,2,128,128]{4,3,2,1,0:T(8,128)}, u32[]{:S(2)}) copy-start(f32[4,2,2,128,128]{4,3,2,1,0:T(8,128)} %copy-done) | copy-start | bytes 3145732
  243.4 8.5 %copy-start.14 = (s32[16]{0:T(128)S(1)}, s32[16]{0:T(128)}, u32[]{:S(2)}) copy-start(s32[16]{0:T(128)} %param.13) | copy-start | bytes 196
  243.4 9.1 %collective-permute-start.3 = (f32[4,2,2,128,128]{4,3,2,1,0:T(8,128)S(1)}, f32[4,2,2,128,128]{4,3,2,1,0:T(8,128)S(1)}, u32[]{:S(2)}, u32[]{:S(2)}) collective-permute-start(f32[4,2,2,128,128]{4,3,2,1,0:T(8,128)S(1)} %shard_map.103.rest_0_), channel_id=1, source_target_pairs={{0,64},{64,0},{1,65},{65,1},{2,66},{66,2},{3,67},{67,3},{4,68},{68... | collective-permute-start | bytes 3145736 | tf_op jit(solution)/shard_map/ppermute | solution.py:347
  251.7 3.1 %collective-permute-start.2 = (f32[4,2,2,128,128]{4,3,2,1,0:T(8,128)S(1)}, f32[4,2,2,128,128]{4,3,2,1,0:T(8,128)S(1)}, u32[]{:S(2)}, u32[]{:S(2)}) collective-permute-start(f32[4,2,2,128,128]{4,3,2,1,0:T(8,128)S(1)} %shard_map.102.rest_1_), channel_id=1, source_target_pairs={{0,64},{64,0},{1,65},{65,1},{2,66},{66,2},{3,67},{67,3},{4,68},{68... | collective-permute-start | bytes 3145736 | tf_op jit(solution)/shard_map/ppermute | solution.py:347

commit v5 on v4

--- a/solution.py
+++ b/solution.py
@@ -67,13 +67,15 @@
     return high, (value - high.astype(F32)).astype(BF16)
 
 
-def collect_kernel(parts, other, local, *rest):
-    kept, done = rest[-1 - len(parts) : -1], rest[-1]
+def collect_kernel(pieces, local, *rest):
+    kept, done = rest[-1 - len(pieces) : -1], rest[-1]
+    half = local.shape[0] // 2
     pool = lax.axis_index("pool")
-    first = local.shape[0] // 2 * (1 - pool if other else pool)
     copies = [
-        pltpu.make_async_copy(local.at[pl.ds(first + start, count)], part, done.at[k])
-        for k, ((start, count), part) in enumerate(zip(parts, kept))
+        pltpu.make_async_copy(
+            local.at[pl.ds(half * (1 - pool if other else pool) + start, count)], part, done.at[k]
+        )
+        for k, ((start, count, other), part) in enumerate(zip(pieces, kept))
     ]
     for copy in copies:
         copy.start()
@@ -266,21 +268,22 @@
     scalars = pl.BlockSpec(memory_space=pltpu.SMEM)
     parts = lambda count: jax.ShapeDtypeStruct((count, *tile), F32)
 
-    def collected(other, share):
+    def collected(pieces, *earlier):
         return pl.pallas_call(
-            functools.partial(collect_kernel, ahead, other),
-            out_shape=tuple(parts(count) for _, count in ahead),
-            in_specs=[far],
-            out_specs=(RESIDENT,) * len(ahead),
-            scratch_shapes=[pltpu.SemaphoreType.DMA((len(ahead),))],
-            compiler_params=limit(share),
+            functools.partial(collect_kernel, pieces),
+            out_shape=tuple(parts(count) for _, count, _ in pieces),
+            in_specs=[far] * (1 + len(earlier)),
+            out_specs=(RESIDENT,) * len(pieces),
+            scratch_shapes=[pltpu.SemaphoreType.DMA((len(pieces),))],
+            compiler_params=limit(49),
             cost_estimate=taking(1),
-        )(local)
-
+        )(local, *earlier)
+
+    (first,) = collected([(*ahead[0], True)])
+    second, *own = collected([(*ahead[1], True), (*ahead[0], False), (*ahead[1], False)], first)
     arrived = []
-    for sent in collected(True, 49):
+    for sent in (first, second):
         arrived.append(lax.ppermute(sent, "pool", swap))
-    own = collected(False, 49)
 
     shape = (devices // 2, 2, planes, mine // 2, 8, n)
     ready = ahead[0][1] // 2
@@ -361,8 +364,8 @@
         )(slot, *arrays, *kept)
 
     starts = [start for start, _ in behind]
-    out = placed([(starts[0], False), (starts[1], False), (starts[0], True)], [*results, others[0]])
-    return placed([(starts[1], True)], [others[1]], out)
+    out = placed([(start, False) for start in starts], results)
+    return placed([(start, True) for start in starts], others, out)
 
 
 def solution(mesh):

time: 257 us -> 257 us (level)
  transfers between devices with their start and end apart: 5 -> 5, of which waited for: 3 -> 4; matrix products, arithmetic and copies ran while one was open for 1% -> 1% of each run, Pallas kernels for 3% -> 3%
where the time goes in v5:
time: 257 us; the launch traced here: 256 us
  blocking collectives  103 us (40%)
  waiting for transfers between devices  94.8 us (37%)
  starting transfers between devices  37.6 us (15%)
  Pallas kernels  18.2 us (7%)
    all_to_all x1, blocking collectives, per_device(): lax.all_to_all(columns.reshape(flat), 'slab', split_axis=0, concat_axis=0...  103 us
    all_to_all x1, waiting for transfers between devices, per_device(): lax.all_to_all(spectrum.reshape(flat), 'slab', split_axis=0, concat_axis=...  93.7 us
    ppermute x2, starting transfers between devices, per_device(): arrived.append(lax.ppermute(sent, 'pool', swap))  20.7 us
    all_to_all x1, starting transfers between devices, per_device(): lax.all_to_all(spectrum.reshape(flat), 'slab', split_axis=0, concat_axis=...  9.91 us
    ppermute x2, starting transfers between devices, per_device(): others.append(lax.ppermute(results[-1], 'pool', swap))  6.9 us
  transfers between devices with their start and end apart: 5, of which 4 were waited for; matrix products, arithmetic and copies ran while one was open for 1% of the time, Pallas kernels for 3%

profile of v5, /device:TPU:33, one launch (start us, length us, event | category | flops | bytes accessed | tf_op | source)
XLA Modules:
  0.0 256.3 jit_solution(17190844524883240761)
XLA Ops:
  0.0 1.2 shard_map.100.rest_0_
  1.3 20.5 %collective-permute-start.1 = (f32[4,2,2,128,128]{4,3,2,1,0:T(8,128)S(1)}, f32[4,2,2,128,128]{4,3,2,1,0:T(8,128)S(1)}, u32[]{:S(2)}, u32[]{:S(2)}) collective-permute-start(f32[4,2,2,128,128]{4,3,2,1,0:T(8,128)S(1)} %shard_map.100.rest_0_), channel_id=1, source_target_pairs={{0,64},{64,0},{1,65},{65,1},{2,66},{66,2},{3,67},{67,3},{4,68},{68... | collective-permute-start | bytes 3145736 | tf_op jit(solution)/shard_map/ppermute | solution.py:286
  21.8 1.9 shard_map.101
  23.7 0.2 collective-permute-start
  23.9 0.2 collective-permute-done.1.arrived
  24.1 2.1 forward0.1.tiles
  26.2 0.3 collective-permute-done.arrived
  26.5 2.9 %forward1.1 = f32[32,2,2,4,8,128]{5,4,3,2,1,0:T(8,128)} custom-call(f32[4,2,2,128,128]{4,3,2,1,0:T(8,128)S(1)} %get-tuple-element.8.own, f32[4,2,2,128,128]{4,3,2,1,0:T(8,128)S(1)} %collective-permute-done.arrived, bf16[2,256,256]{2,1,0:T(8,128)(2,1)S(1)} %copy-done.9, bf16[2,2,256,256]{3,2,1,0:T(8,128)(2,1)S(1)} %copy-done.7, ...), custom_call_target="tpu_custom_call" | custom-call | flops 240000000 | tf_op jit(solution)/shard_map/forward1/pallas_call | solution.py:301
  29.4 9.9 %all-to-all-start = ((f32[64,64,128]{2,1,0:T(8,128)}), f32[64,64,128]{2,1,0:T(8,128)S(1)}, u32[]{:S(2)}, u32[]{:S(2)}) async-start(f32[64,64,128]{2,1,0:T(8,128)} %bitcast.1), calls=%async_computation | async-start | bytes 4194304 | tf_op jit(solution)/shard_map/all_to_all | solution.py:320
  39.4 0.1 add.128
  39.5 0.7 copy.13
  40.2 0.1 broadcast_add_fusion
  40.3 1.0 fusion.kernel
  41.3 93.7 %all-to-all-done = f32[64,64,128]{2,1,0:T(8,128)S(1)} async-done(((f32[64,64,128]{2,1,0:T(8,128)}), f32[64,64,128]{2,1,0:T(8,128)S(1)}, u32[]{:S(2)}, u32[]{:S(2)}) %all-to-all-start) | async-done | bytes 2097184 | tf_op jit(solution)/shard_map/all_to_all | solution.py:320
  135.1 3.4 %middle.1 = f32[128,4,8,128]{3,2,1,0:T(8,128)S(1)} custom-call(f32[128,4,8,128]{3,2,1,0:T(8,128)S(1)} %bitcast.14, bf16[2,2,128,128]{3,2,1,0:T(8,128)(2,1)S(1)} %copy-done.12, bf16[2,2,128,128]{3,2,1,0:T(8,128)(2,1)S(1)} %copy-done.11, f32[2,128,128]{2,1,0:T(8,128)S(1)} %fusion.kernel), custom_call_target="tpu_custom_call" | custom-call | flops 400000000 | tf_op jit(solution)/shard_map/middle/pallas_call | solution.py:322
  138.5 103.3 %all_to_all.10 = f32[64,64,128]{2,1,0:T(8,128)S(1)} all-to-all(f32[64,64,128]{2,1,0:T(8,128)S(1)} %bitcast.15), channel_id=1, replica_groups=mesh['group'=2,'pool'=2,'slab'=64] {'slab'}, dimensions={0} | all-to-all | bytes 4194304 | tf_op jit(solution)/shard_map/all_to_all | solution.py:333
  241.9 1.5 shard_map.102.rest_0_
  243.4 6.7 %collective-permute-start.2 = (f32[4,2,2,128,128]{4,3,2,1,0:T(8,128)S(1)}, f32[4,2,2,128,128]{4,3,2,1,0:T(8,128)S(1)}, u32[]{:S(2)}, u32[]{:S(2)}) collective-permute-start(f32[4,2,2,128,128]{4,3,2,1,0:T(8,128)S(1)} %shard_map.102.rest_0_), channel_id=1, source_target_pairs={{0,64},{64,0},{1,65},{65,1},{2,66},{66,2},{3,67},{67,3},{4,68},{68... | collective-permute-start | bytes 3145736 | tf_op jit(solution)/shard_map/ppermute | solution.py:350
  250.1 1.5 shard_map.103.rest_1_
  251.6 0.2 collective-permute-start.3
  251.7 0.1 select_reduce_fusion.slot
  251.8 1.9 shard_map.104.rest_2_
  253.8 0.5 collective-permute-done.3.rest_1_
  254.3 1.9 shard_map.105
  (36 shorter events, 0.2 us)
Async XLA Ops:
  1.2 22.9 %copy-start.7 = (bf16[2,2,256,256]{3,2,1,0:T(8,128)(2,1)S(1)}, bf16[2,2,256,256]{3,2,1,0:T(8,128)(2,1)}, u32[]{:S(2)}) copy-start(bf16[2,2,256,256]{3,2,1,0:T(8,128)(2,1)} %constant.65.clone.wy) | copy-start | bytes 1572868
  1.3 22.8 %copy-start.9 = (bf16[2,256,256]{2,1,0:T(8,128)(2,1)S(1)}, bf16[2,256,256]{2,1,0:T(8,128)(2,1)}, u32[]{:S(2)}) copy-start(bf16[2,256,256]{2,1,0:T(8,128)(2,1)} %constant.63.clone.wz) | copy-start | bytes 786436
  1.3 22.8 %collective-permute-start.1 = (f32[4,2,2,128,128]{4,3,2,1,0:T(8,128)S(1)}, f32[4,2,2,128,128]{4,3,2,1,0:T(8,128)S(1)}, u32[]{:S(2)}, u32[]{:S(2)}) collective-permute-start(f32[4,2,2,128,128]{4,3,2,1,0:T(8,128)S(1)} %shard_map.100.rest_0_), channel_id=1, source_target_pairs={{0,64},{64,0},{1,65},{65,1},{2,66},{66,2},{3,67},{67,3},{4,68},{68... | collective-permute-start | bytes 3145736 | tf_op jit(solution)/shard_map/ppermute | solution.py:286
  23.7 5.7 %copy-start.4 = (f32[4,2,2,128,128]{4,3,2,1,0:T(8,128)}, f32[4,2,2,128,128]{4,3,2,1,0:T(8,128)S(1)}, u32[]{:S(2)}) copy-start(f32[4,2,2,128,128]{4,3,2,1,0:T(8,128)S(1)} %get-tuple-element.10.own) | copy-start | bytes 3145732
  23.7 2.8 %collective-permute-start = (f32[4,2,2,128,128]{4,3,2,1,0:T(8,128)S(1)}, f32[4,2,2,128,128]{4,3,2,1,0:T(8,128)S(1)}, u32[]{:S(2)}, u32[]{:S(2)}) collective-permute-start(f32[4,2,2,128,128]{4,3,2,1,0:T(8,128)S(1)} %get-tuple-element.9), channel_id=1, source_target_pairs={{0,64},{64,0},{1,65},{65,1},{2,66},{66,2},{3,67},{67,3},{4,68},{68... | collective-permute-start | bytes 3145736 | tf_op jit(solution)/shard_map/ppermute | solution.py:286
  24.1 5.3 %copy-start.2 = (f32[4,2,2,128,128]{4,3,2,1,0:T(8,128)}, f32[4,2,2,128,128]{4,3,2,1,0:T(8,128)S(1)}, u32[]{:S(2)}) copy-start(f32[4,2,2,128,128]{4,3,2,1,0:T(8,128)S(1)} %collective-permute-done.1.arrived) | copy-start | bytes 3145732
  26.5 2.9 %copy-start = (f32[4,2,2,128,128]{4,3,2,1,0:T(8,128)}, f32[4,2,2,128,128]{4,3,2,1,0:T(8,128)S(1)}, u32[]{:S(2)}) copy-start(f32[4,2,2,128,128]{4,3,2,1,0:T(8,128)S(1)} %collective-permute-done.arrived) | copy-start | bytes 3145732
  29.4 10.1 %copy-start.13 = (s32[128,2,128]{2,1,0:T(2,128)S(1)}, s32[128,2,128]{2,1,0:T(2,128)}, u32[]{:S(2)}) copy-start(s32[128,2,128]{2,1,0:T(2,128)} %param.12) | copy-start | bytes 393220
  29.4 105.6 %copy-start.11 = (bf16[2,2,128,128]{3,2,1,0:T(8,128)(2,1)S(1)}, bf16[2,2,128,128]{3,2,1,0:T(8,128)(2,1)}, u32[]{:S(2)}) copy-start(bf16[2,2,128,128]{3,2,1,0:T(8,128)(2,1)} %constant.68.clone.wxi) | copy-start | bytes 393220
  29.4 105.6 %copy-start.12 = (bf16[2,2,128,128]{3,2,1,0:T(8,128)(2,1)S(1)}, bf16[2,2,128,128]{3,2,1,0:T(8,128)(2,1)}, u32[]{:S(2)}) copy-start(bf16[2,2,128,128]{3,2,1,0:T(8,128)(2,1)} %constant.67.clone.wx) | copy-start | bytes 393220
  29.4 105.6 %all-to-all-start = ((f32[64,64,128]{2,1,0:T(8,128)}), f32[64,64,128]{2,1,0:T(8,128)S(1)}, u32[]{:S(2)}, u32[]{:S(2)}) async-start(f32[64,64,128]{2,1,0:T(8,128)} %bitcast.1), calls=%async_computation | async-start | bytes 4194304 | tf_op jit(solution)/shard_map/all_to_all | solution.py:320
  138.5 103.4 %copy-start.3 = (f32[4,2,2,128,128]{4,3,2,1,0:T(8,128)S(1)}, f32[4,2,2,128,128]{4,3,2,1,0:T(8,128)}, u32[]{:S(2)}) copy-start(f32[4,2,2,128,128]{4,3,2,1,0:T(8,128)} %copy-done.2) | copy-start | bytes 3145732
  138.5 103.4 %copy-start.5 = (f32[4,2,2,128,128]{4,3,2,1,0:T(8,128)S(1)}, f32[4,2,2,128,128]{4,3,2,1,0:T(8,128)}, u32[]{:S(2)}) copy-start(f32[4,2,2,128,128]{4,3,2,1,0:T(8,128)} %copy-done.4) | copy-start | bytes 3145732
  138.5 103.4 %copy-start.6 = (bf16[2,2,256,256]{3,2,1,0:T(8,128)(2,1)S(1)}, bf16[2,2,256,256]{3,2,1,0:T(8,128)(2,1)}, u32[]{:S(2)}) copy-start(bf16[2,2,256,256]{3,2,1,0:T(8,128)(2,1)} %constant.66.clone.wyi) | copy-start | bytes 1572868
  138.5 103.3 %copy-start.8 = (bf16[2,256,256]{2,1,0:T(8,128)(2,1)S(1)}, bf16[2,256,256]{2,1,0:T(8,128)(2,1)}, u32[]{:S(2)}) copy-start(bf16[2,256,256]{2,1,0:T(8,128)(2,1)} %constant.64.clone.wzi) | copy-start | bytes 786436
  138.5 103.3 %copy-start.10 = (f32[2,128,128]{2,1,0:T(8,128)S(1)}, f32[2,128,128]{2,1,0:T(8,128)}, u32[]{:S(2)}) copy-start(f32[2,128,128]{2,1,0:T(8,128)} %fxc.3) | copy-start | bytes 393220
  241.9 8.2 %copy-start.1 = (f32[4,2,2,128,128]{4,3,2,1,0:T(8,128)S(1)}, f32[4,2,2,128,128]{4,3,2,1,0:T(8,128)}, u32[]{:S(2)}) copy-start(f32[4,2,2,128,128]{4,3,2,1,0:T(8,128)} %copy-done) | copy-start | bytes 3145732
  243.4 8.4 %copy-start.14 = (s32[16]{0:T(128)S(1)}, s32[16]{0:T(128)}, u32[]{:S(2)}) copy-start(s32[16]{0:T(128)} %param.13) | copy-start | bytes 196
  243.4 10.4 %collective-permute-start.2 = (f32[4,2,2,128,128]{4,3,2,1,0:T(8,128)S(1)}, f32[4,2,2,128,128]{4,3,2,1,0:T(8,128)S(1)}, u32[]{:S(2)}, u32[]{:S(2)}) collective-permute-start(f32[4,2,2,128,128]{4,3,2,1,0:T(8,128)S(1)} %shard_map.102.rest_0_), channel_id=1, source_target_pairs={{0,64},{64,0},{1,65},{65,1},{2,66},{66,2},{3,67},{67,3},{4,68},{68... | collective-permute-start | bytes 3145736 | tf_op jit(solution)/shard_map/ppermute | solution.py:350
  251.6 2.8 %collective-permute-start.3 = (f32[4,2,2,128,128]{4,3,2,1,0:T(8,128)S(1)}, f32[4,2,2,128,128]{4,3,2,1,0:T(8,128)S(1)}, u32[]{:S(2)}, u32[]{:S(2)}) collective-permute-start(f32[4,2,2,128,128]{4,3,2,1,0:T(8,128)S(1)} %shard_map.103.rest_1_), channel_id=1, source_target_pairs={{0,64},{64,0},{1,65},{65,1},{2,66},{66,2},{3,67},{67,3},{4,68},{68... | collective-permute-start | bytes 3145736 | tf_op jit(solution)/shard_map/ppermute | solution.py:350

commit v6 on v5

--- a/solution.py
+++ b/solution.py
@@ -159,8 +159,9 @@
     length = kernel.shape[1]
     half = length // 2
     step = pl.program_id(0)
-    rows[...] = columns[:, step].reshape(rows.shape)
-    grab = lambda j: rows[pl.ds(j, length, stride=8), :]
+    for x in range(length):
+        rows[pl.ds(PITCH * x, 8), :] = columns[x, step]
+    grab = lambda j: rows[pl.ds(j, length, stride=PITCH), :]
     order = [(p, b) for p in range(2) for b in range(2)]
     fields = [jnp.concatenate([grab(4 * p + 2 * r + b) for p, b in order], axis=1) for r in range(2)]
     total = jnp.concatenate([f[:half] + f[half:] for f in fields], axis=0)
@@ -175,10 +176,11 @@
     for i, (p, b) in enumerate(order):
         for r in range(2):
             for h, side in enumerate(sides):
-                back[pl.ds(h * half * 8 + 4 * p + 2 * r + b, half, stride=8), :] = side[
+                back[pl.ds(h * half * PITCH + 4 * p + 2 * r + b, half, stride=PITCH), :] = side[
                     r * half : (r + 1) * half, i * n : (i + 1) * n
                 ]
-    out[:, step] = back[...].reshape(length, 8, n)
+    for x in range(length):
+        out[x, step] = back[pl.ds(PITCH * x, 8), :]
 
 
 def backward_kernel(start, columns, wyi, wzi, fxc, own, arrived, out):
@@ -237,6 +239,7 @@
 
 
 RESIDENT = pl.BlockSpec(memory_space=pltpu.VMEM)
+PITCH = 9
 
 
 def taking(us):
@@ -325,7 +328,7 @@
         grid=(mine // 2,),
         in_specs=[RESIDENT] * 4,
         out_specs=RESIDENT,
-        scratch_shapes=[pltpu.VMEM((n * 8, n), F32), pltpu.VMEM((n * 8, n), F32)],
+        scratch_shapes=[pltpu.VMEM((n * PITCH, n), F32)] * 2,
         compiler_params=limit(40),
         cost_estimate=taking(4),
         name="middle",

time: 257 us -> 256 us (level)
  no operation moved by 1% of the time
where the time goes in v6:
time: 256 us
  blocking collectives  103 us (40%)
  waiting for transfers between devices  94.8 us (37%)
  starting transfers between devices  37.6 us (15%)
  Pallas kernels  17.9 us (7%)
    all_to_all x1, blocking collectives, per_device(): lax.all_to_all(columns.reshape(flat), 'slab', split_axis=0, concat_axis=0...  103 us
    all_to_all x1, waiting for transfers between devices, per_device(): lax.all_to_all(spectrum.reshape(flat), 'slab', split_axis=0, concat_axis=...  93.7 us
    ppermute x2, starting transfers between devices, per_device(): arrived.append(lax.ppermute(sent, 'pool', swap))  20.7 us
    all_to_all x1, starting transfers between devices, per_device(): lax.all_to_all(spectrum.reshape(flat), 'slab', split_axis=0, concat_axis=...  9.91 us
    ppermute x2, starting transfers between devices, per_device(): others.append(lax.ppermute(results[-1], 'pool', swap))  6.89 us
  transfers between devices with their start and end apart: 5, of which 4 were waited for; matrix products, arithmetic and copies ran while one was open for 1% of the time, Pallas kernels for 3%

profile of v6, /device:TPU:33, one launch (start us, length us, event | category | flops | bytes accessed | tf_op | source)
XLA Modules:
  0.0 255.9 jit_solution(2316299383078931395)
XLA Ops:
  0.0 1.2 shard_map.100.rest_0_
  1.3 20.5 %collective-permute-start.1 = (f32[4,2,2,128,128]{4,3,2,1,0:T(8,128)S(1)}, f32[4,2,2,128,128]{4,3,2,1,0:T(8,128)S(1)}, u32[]{:S(2)}, u32[]{:S(2)}) collective-permute-start(f32[4,2,2,128,128]{4,3,2,1,0:T(8,128)S(1)} %shard_map.100.rest_0_), channel_id=1, source_target_pairs={{0,64},{64,0},{1,65},{65,1},{2,66},{66,2},{3,67},{67,3},{4,68},{68... | collective-permute-start | bytes 3145736 | tf_op jit(solution)/shard_map/ppermute | solution.py:289
  21.8 1.9 shard_map.101
  23.7 0.2 collective-permute-start
  23.9 0.2 collective-permute-done.1.arrived
  24.1 2.1 forward0.1.tiles
  26.2 0.3 collective-permute-done.arrived
  26.5 2.9 %forward1.1 = f32[32,2,2,4,8,128]{5,4,3,2,1,0:T(8,128)} custom-call(f32[4,2,2,128,128]{4,3,2,1,0:T(8,128)S(1)} %get-tuple-element.8.own, f32[4,2,2,128,128]{4,3,2,1,0:T(8,128)S(1)} %collective-permute-done.arrived, bf16[2,256,256]{2,1,0:T(8,128)(2,1)S(1)} %copy-done.9, bf16[2,2,256,256]{3,2,1,0:T(8,128)(2,1)S(1)} %copy-done.7, ...), custom_call_target="tpu_custom_call" | custom-call | flops 240000000 | tf_op jit(solution)/shard_map/forward1/pallas_call | solution.py:304
  29.4 9.9 %all-to-all-start = ((f32[64,64,128]{2,1,0:T(8,128)}), f32[64,64,128]{2,1,0:T(8,128)S(1)}, u32[]{:S(2)}, u32[]{:S(2)}) async-start(f32[64,64,128]{2,1,0:T(8,128)} %bitcast.1), calls=%async_computation | async-start | bytes 4194304 | tf_op jit(solution)/shard_map/all_to_all | solution.py:323
  39.4 0.1 add.128
  39.5 0.7 copy.13
  40.2 0.1 broadcast_add_fusion
  40.3 1.0 fusion.kernel
  41.3 93.7 %all-to-all-done = f32[64,64,128]{2,1,0:T(8,128)S(1)} async-done(((f32[64,64,128]{2,1,0:T(8,128)}), f32[64,64,128]{2,1,0:T(8,128)S(1)}, u32[]{:S(2)}, u32[]{:S(2)}) %all-to-all-start) | async-done | bytes 2097184 | tf_op jit(solution)/shard_map/all_to_all | solution.py:323
  135.1 3.0 %middle.1 = f32[128,4,8,128]{3,2,1,0:T(8,128)S(1)} custom-call(f32[128,4,8,128]{3,2,1,0:T(8,128)S(1)} %bitcast.14, bf16[2,2,128,128]{3,2,1,0:T(8,128)(2,1)S(1)} %copy-done.12, bf16[2,2,128,128]{3,2,1,0:T(8,128)(2,1)S(1)} %copy-done.11, f32[2,128,128]{2,1,0:T(8,128)S(1)} %fusion.kernel), custom_call_target="tpu_custom_call" | custom-call | flops 400000000 | tf_op jit(solution)/shard_map/middle/pallas_call | solution.py:325
  138.1 103.3 %all_to_all.10 = f32[64,64,128]{2,1,0:T(8,128)S(1)} all-to-all(f32[64,64,128]{2,1,0:T(8,128)S(1)} %bitcast.15), channel_id=1, replica_groups=mesh['group'=2,'pool'=2,'slab'=64] {'slab'}, dimensions={0} | all-to-all | bytes 4194304 | tf_op jit(solution)/shard_map/all_to_all | solution.py:336
  241.5 1.5 shard_map.102.rest_0_
  243.0 6.7 %collective-permute-start.2 = (f32[4,2,2,128,128]{4,3,2,1,0:T(8,128)S(1)}, f32[4,2,2,128,128]{4,3,2,1,0:T(8,128)S(1)}, u32[]{:S(2)}, u32[]{:S(2)}) collective-permute-start(f32[4,2,2,128,128]{4,3,2,1,0:T(8,128)S(1)} %shard_map.102.rest_0_), channel_id=1, source_target_pairs={{0,64},{64,0},{1,65},{65,1},{2,66},{66,2},{3,67},{67,3},{4,68},{68... | collective-permute-start | bytes 3145736 | tf_op jit(solution)/shard_map/ppermute | solution.py:353
  249.7 1.5 shard_map.103.rest_1_
  251.2 0.2 collective-permute-start.3
  251.4 0.1 select_reduce_fusion.slot
  251.5 1.9 shard_map.104.rest_2_
  253.4 0.5 collective-permute-done.3.rest_1_
  254.0 1.9 shard_map.105
  (36 shorter events, 0.2 us)
Async XLA Ops:
  1.2 22.9 %copy-start.7 = (bf16[2,2,256,256]{3,2,1,0:T(8,128)(2,1)S(1)}, bf16[2,2,256,256]{3,2,1,0:T(8,128)(2,1)}, u32[]{:S(2)}) copy-start(bf16[2,2,256,256]{3,2,1,0:T(8,128)(2,1)} %constant.65.clone.wy) | copy-start | bytes 1572868
  1.3 22.8 %copy-start.9 = (bf16[2,256,256]{2,1,0:T(8,128)(2,1)S(1)}, bf16[2,256,256]{2,1,0:T(8,128)(2,1)}, u32[]{:S(2)}) copy-start(bf16[2,256,256]{2,1,0:T(8,128)(2,1)} %constant.63.clone.wz) | copy-start | bytes 786436
  1.3 22.8 %collective-permute-start.1 = (f32[4,2,2,128,128]{4,3,2,1,0:T(8,128)S(1)}, f32[4,2,2,128,128]{4,3,2,1,0:T(8,128)S(1)}, u32[]{:S(2)}, u32[]{:S(2)}) collective-permute-start(f32[4,2,2,128,128]{4,3,2,1,0:T(8,128)S(1)} %shard_map.100.rest_0_), channel_id=1, source_target_pairs={{0,64},{64,0},{1,65},{65,1},{2,66},{66,2},{3,67},{67,3},{4,68},{68... | collective-permute-start | bytes 3145736 | tf_op jit(solution)/shard_map/ppermute | solution.py:289
  23.7 5.7 %copy-start.4 = (f32[4,2,2,128,128]{4,3,2,1,0:T(8,128)}, f32[4,2,2,128,128]{4,3,2,1,0:T(8,128)S(1)}, u32[]{:S(2)}) copy-start(f32[4,2,2,128,128]{4,3,2,1,0:T(8,128)S(1)} %get-tuple-element.10.own) | copy-start | bytes 3145732
  23.7 2.8 %collective-permute-start = (f32[4,2,2,128,128]{4,3,2,1,0:T(8,128)S(1)}, f32[4,2,2,128,128]{4,3,2,1,0:T(8,128)S(1)}, u32[]{:S(2)}, u32[]{:S(2)}) collective-permute-start(f32[4,2,2,128,128]{4,3,2,1,0:T(8,128)S(1)} %get-tuple-element.9), channel_id=1, source_target_pairs={{0,64},{64,0},{1,65},{65,1},{2,66},{66,2},{3,67},{67,3},{4,68},{68... | collective-permute-start | bytes 3145736 | tf_op jit(solution)/shard_map/ppermute | solution.py:289
  24.1 5.3 %copy-start.2 = (f32[4,2,2,128,128]{4,3,2,1,0:T(8,128)}, f32[4,2,2,128,128]{4,3,2,1,0:T(8,128)S(1)}, u32[]{:S(2)}) copy-start(f32[4,2,2,128,128]{4,3,2,1,0:T(8,128)S(1)} %collective-permute-done.1.arrived) | copy-start | bytes 3145732
  26.5 2.9 %copy-start = (f32[4,2,2,128,128]{4,3,2,1,0:T(8,128)}, f32[4,2,2,128,128]{4,3,2,1,0:T(8,128)S(1)}, u32[]{:S(2)}) copy-start(f32[4,2,2,128,128]{4,3,2,1,0:T(8,128)S(1)} %collective-permute-done.arrived) | copy-start | bytes 3145732
  29.4 10.1 %copy-start.13 = (s32[128,2,128]{2,1,0:T(2,128)S(1)}, s32[128,2,128]{2,1,0:T(2,128)}, u32[]{:S(2)}) copy-start(s32[128,2,128]{2,1,0:T(2,128)} %param.12) | copy-start | bytes 393220
  29.4 105.6 %copy-start.11 = (bf16[2,2,128,128]{3,2,1,0:T(8,128)(2,1)S(1)}, bf16[2,2,128,128]{3,2,1,0:T(8,128)(2,1)}, u32[]{:S(2)}) copy-start(bf16[2,2,128,128]{3,2,1,0:T(8,128)(2,1)} %constant.68.clone.wxi) | copy-start | bytes 393220
  29.4 105.6 %copy-start.12 = (bf16[2,2,128,128]{3,2,1,0:T(8,128)(2,1)S(1)}, bf16[2,2,128,128]{3,2,1,0:T(8,128)(2,1)}, u32[]{:S(2)}) copy-start(bf16[2,2,128,128]{3,2,1,0:T(8,128)(2,1)} %constant.67.clone.wx) | copy-start | bytes 393220
  29.4 105.6 %all-to-all-start = ((f32[64,64,128]{2,1,0:T(8,128)}), f32[64,64,128]{2,1,0:T(8,128)S(1)}, u32[]{:S(2)}, u32[]{:S(2)}) async-start(f32[64,64,128]{2,1,0:T(8,128)} %bitcast.1), calls=%async_computation | async-start | bytes 4194304 | tf_op jit(solution)/shard_map/all_to_all | solution.py:323
  138.1 103.4 %copy-start.3 = (f32[4,2,2,128,128]{4,3,2,1,0:T(8,128)S(1)}, f32[4,2,2,128,128]{4,3,2,1,0:T(8,128)}, u32[]{:S(2)}) copy-start(f32[4,2,2,128,128]{4,3,2,1,0:T(8,128)} %copy-done.2) | copy-start | bytes 3145732
  138.1 103.4 %copy-start.5 = (f32[4,2,2,128,128]{4,3,2,1,0:T(8,128)S(1)}, f32[4,2,2,128,128]{4,3,2,1,0:T(8,128)}, u32[]{:S(2)}) copy-start(f32[4,2,2,128,128]{4,3,2,1,0:T(8,128)} %copy-done.4) | copy-start | bytes 3145732
  138.1 103.4 %copy-start.6 = (bf16[2,2,256,256]{3,2,1,0:T(8,128)(2,1)S(1)}, bf16[2,2,256,256]{3,2,1,0:T(8,128)(2,1)}, u32[]{:S(2)}) copy-start(bf16[2,2,256,256]{3,2,1,0:T(8,128)(2,1)} %constant.66.clone.wyi) | copy-start | bytes 1572868
  138.1 103.4 %copy-start.8 = (bf16[2,256,256]{2,1,0:T(8,128)(2,1)S(1)}, bf16[2,256,256]{2,1,0:T(8,128)(2,1)}, u32[]{:S(2)}) copy-start(bf16[2,256,256]{2,1,0:T(8,128)(2,1)} %constant.64.clone.wzi) | copy-start | bytes 786436
  138.1 103.4 %copy-start.10 = (f32[2,128,128]{2,1,0:T(8,128)S(1)}, f32[2,128,128]{2,1,0:T(8,128)}, u32[]{:S(2)}) copy-start(f32[2,128,128]{2,1,0:T(8,128)} %fxc.3) | copy-start | bytes 393220
  241.5 8.2 %copy-start.1 = (f32[4,2,2,128,128]{4,3,2,1,0:T(8,128)S(1)}, f32[4,2,2,128,128]{4,3,2,1,0:T(8,128)}, u32[]{:S(2)}) copy-start(f32[4,2,2,128,128]{4,3,2,1,0:T(8,128)} %copy-done) | copy-start | bytes 3145732
  243.0 8.4 %copy-start.14 = (s32[16]{0:T(128)S(1)}, s32[16]{0:T(128)}, u32[]{:S(2)}) copy-start(s32[16]{0:T(128)} %param.13) | copy-start | bytes 196
  243.0 10.4 %collective-permute-start.2 = (f32[4,2,2,128,128]{4,3,2,1,0:T(8,128)S(1)}, f32[4,2,2,128,128]{4,3,2,1,0:T(8,128)S(1)}, u32[]{:S(2)}, u32[]{:S(2)}) collective-permute-start(f32[4,2,2,128,128]{4,3,2,1,0:T(8,128)S(1)} %shard_map.102.rest_0_), channel_id=1, source_target_pairs={{0,64},{64,0},{1,65},{65,1},{2,66},{66,2},{3,67},{67,3},{4,68},{68... | collective-permute-start | bytes 3145736 | tf_op jit(solution)/shard_map/ppermute | solution.py:353
  251.2 2.8 %collective-permute-start.3 = (f32[4,2,2,128,128]{4,3,2,1,0:T(8,128)S(1)}, f32[4,2,2,128,128]{4,3,2,1,0:T(8,128)S(1)}, u32[]{:S(2)}, u32[]{:S(2)}) collective-permute-start(f32[4,2,2,128,128]{4,3,2,1,0:T(8,128)S(1)} %shard_map.103.rest_1_), channel_id=1, source_target_pairs={{0,64},{64,0},{1,65},{65,1},{2,66},{66,2},{3,67},{67,3},{4,68},{68... | collective-permute-start | bytes 3145736 | tf_op jit(solution)/shard_map/ppermute | solution.py:353

commit v7 on v5

--- a/solution.py
+++ b/solution.py
@@ -98,13 +98,24 @@
     return jnp.where(lower, even, odd), jnp.where(lower, odd, even)
 
 
-def forward_first_kernel(own, arrived, wz, wy, tiles):
+def forward_first_kernel(start, own, arrived, wz, wy, local, tiles, own_next, done):
     n = own.shape[-1]
     step = pl.program_id(0)
+    first = local.shape[0] // 2 * lax.axis_index("pool") + start
+    fetch = pltpu.make_async_copy(local.at[pl.ds(first, own_next.shape[0])], own_next, done)
+
+    @pl.when(step == 0)
+    def _():
+        fetch.start()
+
     pair = pl.ds(2 * step, 2)
     for j, value in enumerate(transformed(own[pair] + arrived[pair], wz[...], wy[...])):
         for a in range(2):
             tiles[:, j, a, step] = value[:, :, a * n : (a + 1) * n]
+
+    @pl.when(step == pl.num_programs(0) - 1)
+    def _():
+        fetch.wait()
 
 
 def forward_second_kernel(own, arrived, wz, wy, tiles, spectrum, later, done):
@@ -159,26 +170,31 @@
     length = kernel.shape[1]
     half = length // 2
     step = pl.program_id(0)
-    rows[...] = columns[:, step].reshape(rows.shape)
-    grab = lambda j: rows[pl.ds(j, length, stride=8), :]
-    order = [(p, b) for p in range(2) for b in range(2)]
-    fields = [jnp.concatenate([grab(4 * p + 2 * r + b) for p, b in order], axis=1) for r in range(2)]
+    pairs = rows.shape[0]
+    for m in range(pairs):
+        for x in range(length):
+            rows[m, pl.ds(PITCH * x, 8), :] = columns[x, pairs * step + m]
+    order = [(m, p, b) for m in range(pairs) for p in range(2) for b in range(2)]
+    grab = lambda m, j: rows[m, pl.ds(j, length, stride=PITCH), :]
+    fields = [jnp.concatenate([grab(m, 4 * p + 2 * r + b) for m, p, b in order], axis=1) for r in range(2)]
     total = jnp.concatenate([f[:half] + f[half:] for f in fields], axis=0)
     difference = jnp.concatenate([f[:half] - f[half:] for f in fields], axis=0)
     spectrum = by_parts(wx, total, difference)
-    both = jnp.concatenate([kernel[0], kernel[1]] * 2, axis=1)
+    both = jnp.concatenate([kernel[0], kernel[1]] * (2 * pairs), axis=1)
     both = jnp.concatenate([both[:half], both[:half], both[half:], both[half:]], axis=0)
     spectrum = spectrum * both
     result = by_parts(wxi, spectrum[:length], spectrum[length:])
     even, odd = result[:length], result[length:]
     sides = (even + odd, even - odd)
-    for i, (p, b) in enumerate(order):
+    for i, (m, p, b) in enumerate(order):
         for r in range(2):
             for h, side in enumerate(sides):
-                back[pl.ds(h * half * 8 + 4 * p + 2 * r + b, half, stride=8), :] = side[
+                back[m, pl.ds(h * half * PITCH + 4 * p + 2 * r + b, half, stride=PITCH), :] = side[
                     r * half : (r + 1) * half, i * n : (i + 1) * n
                 ]
-    out[:, step] = back[...].reshape(length, 8, n)
+    for m in range(pairs):
+        for x in range(length):
+            out[x, pairs * step + m] = back[m, pl.ds(PITCH * x, 8), :]
 
 
 def backward_kernel(start, columns, wyi, wzi, fxc, own, arrived, out):
@@ -237,6 +253,7 @@
 
 
 RESIDENT = pl.BlockSpec(memory_space=pltpu.VMEM)
+PITCH = 9
 
 
 def taking(us):
@@ -280,23 +297,25 @@
         )(local, *earlier)
 
     (first,) = collected([(*ahead[0], True)])
-    second, *own = collected([(*ahead[1], True), (*ahead[0], False), (*ahead[1], False)], first)
+    second, own_first = collected([(*ahead[1], True), (*ahead[0], False)], first)
     arrived = []
     for sent in (first, second):
         arrived.append(lax.ppermute(sent, "pool", swap))
 
     shape = (devices // 2, 2, planes, mine // 2, 8, n)
     ready = ahead[0][1] // 2
-    tiles = pl.pallas_call(
-        forward_first_kernel,
-        out_shape=jax.ShapeDtypeStruct((*shape[:3], ready, *shape[4:]), F32),
+    tiles, own_second = pl.pallas_call(
+        functools.partial(forward_first_kernel, ahead[1][0]),
+        out_shape=(jax.ShapeDtypeStruct((*shape[:3], ready, *shape[4:]), F32), parts(ahead[1][1])),
         grid=(ready,),
-        in_specs=[RESIDENT] * 4,
-        out_specs=RESIDENT,
-        compiler_params=limit(40),
+        in_specs=[RESIDENT] * 4 + [far],
+        out_specs=(RESIDENT, RESIDENT),
+        scratch_shapes=[pltpu.SemaphoreType.DMA],
+        compiler_params=limit(49),
         cost_estimate=taking(2.4),
         name="forward0",
-    )(own[0], arrived[0], wz, wy)
+    )(own_first, arrived[0], wz, wy, local)
+    own = [own_first, own_second]
     later = shape[3] - ready
     spectrum = pl.pallas_call(
         forward_second_kernel,
@@ -322,10 +341,10 @@
     columns = pl.pallas_call(
         middle_kernel,
         out_shape=jax.ShapeDtypeStruct(columns.shape, F32),
-        grid=(mine // 2,),
+        grid=(mine // 4,),
         in_specs=[RESIDENT] * 4,
         out_specs=RESIDENT,
-        scratch_shapes=[pltpu.VMEM((n * 8, n), F32), pltpu.VMEM((n * 8, n), F32)],
+        scratch_shapes=[pltpu.VMEM((2, n * PITCH, n), F32)] * 2,
         compiler_params=limit(40),
         cost_estimate=taking(4),
         name="middle",

time: 257 us -> 255 us (level)
  transfers between devices with their start and end apart: 5 -> 5, of which waited for: 4 -> 3; matrix products, arithmetic and copies ran while one was open for 1% -> 1% of each run, Pallas kernels for 3% -> 3%
where the time goes in v7:
time: 255 us
  blocking collectives  104 us (41%)
  waiting for transfers between devices  94.2 us (37%)
  starting transfers between devices  37.7 us (15%)
  Pallas kernels  16.9 us (7%)
    all_to_all x1, blocking collectives, per_device(): lax.all_to_all(columns.reshape(flat), 'slab', split_axis=0, concat_axis=0...  104 us
    all_to_all x1, waiting for transfers between devices, per_device(): lax.all_to_all(spectrum.reshape(flat), 'slab', split_axis=0, concat_axis=...  93.2 us
    ppermute x2, starting transfers between devices, per_device(): arrived.append(lax.ppermute(sent, 'pool', swap))  20.7 us
    all_to_all x1, starting transfers between devices, per_device(): lax.all_to_all(spectrum.reshape(flat), 'slab', split_axis=0, concat_axis=...  9.91 us
    ppermute x2, starting transfers between devices, per_device(): others.append(lax.ppermute(results[-1], 'pool', swap))  7 us
  transfers between devices with their start and end apart: 5, of which 3 were waited for; matrix products, arithmetic and copies ran while one was open for 1% of the time, Pallas kernels for 3%

profile of v7, /device:TPU:33, one launch (start us, length us, event | category | flops | bytes accessed | tf_op | source)
XLA Modules:
  0.0 254.9 jit_solution(10889402887931425550)
XLA Ops:
  0.0 1.2 shard_map.100.rest_0_
  1.3 20.5 %collective-permute-start = (f32[4,2,2,128,128]{4,3,2,1,0:T(8,128)S(1)}, f32[4,2,2,128,128]{4,3,2,1,0:T(8,128)S(1)}, u32[]{:S(2)}, u32[]{:S(2)}) collective-permute-start(f32[4,2,2,128,128]{4,3,2,1,0:T(8,128)S(1)} %shard_map.100.rest_0_), channel_id=1, source_target_pairs={{0,64},{64,0},{1,65},{65,1},{2,66},{66,2},{3,67},{67,3},{4,68},{68... | collective-permute-start | bytes 3145736 | tf_op jit(solution)/shard_map/ppermute | solution.py:303
  21.8 1.6 shard_map.101
  23.4 0.2 collective-permute-start.1
  23.6 0.5 collective-permute-done.arrived
  24.1 2.1 forward0.1
  26.2 2.9 %forward1.1 = f32[32,2,2,4,8,128]{5,4,3,2,1,0:T(8,128)} custom-call(f32[4,2,2,128,128]{4,3,2,1,0:T(8,128)S(1)} %get-tuple-element.10.own, f32[4,2,2,128,128]{4,3,2,1,0:T(8,128)S(1)} %collective-permute-done.1.arrived, bf16[2,256,256]{2,1,0:T(8,128)(2,1)S(1)} %copy-done.8, bf16[2,2,256,256]{3,2,1,0:T(8,128)(2,1)S(1)} %copy-done.7, ...), custom_call_target="tpu_custom_call" | custom-call | flops 240000000 | tf_op jit(solution)/shard_map/forward1/pallas_call | solution.py:320
  29.2 9.9 %all-to-all-start = ((f32[64,64,128]{2,1,0:T(8,128)}), f32[64,64,128]{2,1,0:T(8,128)S(1)}, u32[]{:S(2)}, u32[]{:S(2)}) async-start(f32[64,64,128]{2,1,0:T(8,128)} %bitcast.1), calls=%async_computation | async-start | bytes 4194304 | tf_op jit(solution)/shard_map/all_to_all | solution.py:339
  39.1 0.1 add.128
  39.2 0.1 convert_multiply_fusion
  39.3 0.7 copy.13
  40.0 0.1 broadcast_add_fusion
  40.0 1.0 fusion.kernel
  41.0 93.2 %all-to-all-done = f32[64,64,128]{2,1,0:T(8,128)S(1)} async-done(((f32[64,64,128]{2,1,0:T(8,128)}), f32[64,64,128]{2,1,0:T(8,128)S(1)}, u32[]{:S(2)}, u32[]{:S(2)}) %all-to-all-start) | async-done | bytes 2097184 | tf_op jit(solution)/shard_map/all_to_all | solution.py:339
  134.2 2.3 middle.1
  136.6 103.7 %all_to_all.10 = f32[64,64,128]{2,1,0:T(8,128)S(1)} all-to-all(f32[64,64,128]{2,1,0:T(8,128)S(1)} %bitcast.15), channel_id=1, replica_groups=mesh['group'=2,'pool'=2,'slab'=64] {'slab'}, dimensions={0} | all-to-all | bytes 4194304 | tf_op jit(solution)/shard_map/all_to_all | solution.py:352
  240.4 1.5 shard_map.102.rest_0_
  241.9 6.8 %collective-permute-start.2 = (f32[4,2,2,128,128]{4,3,2,1,0:T(8,128)S(1)}, f32[4,2,2,128,128]{4,3,2,1,0:T(8,128)S(1)}, u32[]{:S(2)}, u32[]{:S(2)}) collective-permute-start(f32[4,2,2,128,128]{4,3,2,1,0:T(8,128)S(1)} %shard_map.102.rest_0_), channel_id=1, source_target_pairs={{0,64},{64,0},{1,65},{65,1},{2,66},{66,2},{3,67},{67,3},{4,68},{68... | collective-permute-start | bytes 3145736 | tf_op jit(solution)/shard_map/ppermute | solution.py:369
  248.7 1.5 shard_map.103.rest_1_
  250.2 0.2 collective-permute-start.3
  250.4 0.1 select_reduce_fusion.slot
  250.5 1.9 shard_map.104.rest_2_
  252.4 0.5 collective-permute-done.3.rest_1_
  253.0 1.9 shard_map.105
  (36 shorter events, 0.1 us)
Async XLA Ops:
  1.2 22.9 %copy-start.7 = (bf16[2,2,256,256]{3,2,1,0:T(8,128)(2,1)S(1)}, bf16[2,2,256,256]{3,2,1,0:T(8,128)(2,1)}, u32[]{:S(2)}) copy-start(bf16[2,2,256,256]{3,2,1,0:T(8,128)(2,1)} %constant.65.clone.wy) | copy-start | bytes 1572868
  1.3 22.8 %copy-start.8 = (bf16[2,256,256]{2,1,0:T(8,128)(2,1)S(1)}, bf16[2,256,256]{2,1,0:T(8,128)(2,1)}, u32[]{:S(2)}) copy-start(bf16[2,256,256]{2,1,0:T(8,128)(2,1)} %constant.63.clone.wz) | copy-start | bytes 786436
  1.3 22.8 %collective-permute-start = (f32[4,2,2,128,128]{4,3,2,1,0:T(8,128)S(1)}, f32[4,2,2,128,128]{4,3,2,1,0:T(8,128)S(1)}, u32[]{:S(2)}, u32[]{:S(2)}) collective-permute-start(f32[4,2,2,128,128]{4,3,2,1,0:T(8,128)S(1)} %shard_map.100.rest_0_), channel_id=1, source_target_pairs={{0,64},{64,0},{1,65},{65,1},{2,66},{66,2},{3,67},{67,3},{4,68},{68... | collective-permute-start | bytes 3145736 | tf_op jit(solution)/shard_map/ppermute | solution.py:303
  23.4 2.8 %copy-start = (f32[4,2,2,128,128]{4,3,2,1,0:T(8,128)}, f32[4,2,2,128,128]{4,3,2,1,0:T(8,128)S(1)}, u32[]{:S(2)}) copy-start(f32[4,2,2,128,128]{4,3,2,1,0:T(8,128)S(1)} %get-tuple-element.9.own) | copy-start | bytes 3145732
  23.4 2.8 %collective-permute-start.1 = (f32[4,2,2,128,128]{4,3,2,1,0:T(8,128)S(1)}, f32[4,2,2,128,128]{4,3,2,1,0:T(8,128)S(1)}, u32[]{:S(2)}, u32[]{:S(2)}) collective-permute-start(f32[4,2,2,128,128]{4,3,2,1,0:T(8,128)S(1)} %get-tuple-element.11), channel_id=1, source_target_pairs={{0,64},{64,0},{1,65},{65,1},{2,66},{66,2},{3,67},{67,3},{4,68},{68... | collective-permute-start | bytes 3145736 | tf_op jit(solution)/shard_map/ppermute | solution.py:303
  26.2 2.9 %copy-start.4 = (f32[4,2,2,128,128]{4,3,2,1,0:T(8,128)}, f32[4,2,2,128,128]{4,3,2,1,0:T(8,128)S(1)}, u32[]{:S(2)}) copy-start(f32[4,2,2,128,128]{4,3,2,1,0:T(8,128)S(1)} %get-tuple-element.10.own) | copy-start | bytes 3145732
  26.2 2.9 %copy-start.2 = (f32[4,2,2,128,128]{4,3,2,1,0:T(8,128)}, f32[4,2,2,128,128]{4,3,2,1,0:T(8,128)S(1)}, u32[]{:S(2)}) copy-start(f32[4,2,2,128,128]{4,3,2,1,0:T(8,128)S(1)} %collective-permute-done.1.arrived) | copy-start | bytes 3145732
  29.1 10.1 %copy-start.13 = (s32[128,2,128]{2,1,0:T(2,128)S(1)}, s32[128,2,128]{2,1,0:T(2,128)}, u32[]{:S(2)}) copy-start(s32[128,2,128]{2,1,0:T(2,128)} %param.12) | copy-start | bytes 393220
  29.1 105.1 %copy-start.11 = (bf16[2,2,128,128]{3,2,1,0:T(8,128)(2,1)S(1)}, bf16[2,2,128,128]{3,2,1,0:T(8,128)(2,1)}, u32[]{:S(2)}) copy-start(bf16[2,2,128,128]{3,2,1,0:T(8,128)(2,1)} %constant.68.clone.wxi) | copy-start | bytes 393220
  29.1 105.1 %copy-start.12 = (bf16[2,2,128,128]{3,2,1,0:T(8,128)(2,1)S(1)}, bf16[2,2,128,128]{3,2,1,0:T(8,128)(2,1)}, u32[]{:S(2)}) copy-start(bf16[2,2,128,128]{3,2,1,0:T(8,128)(2,1)} %constant.67.clone.wx) | copy-start | bytes 393220
  29.2 105.1 %all-to-all-start = ((f32[64,64,128]{2,1,0:T(8,128)}), f32[64,64,128]{2,1,0:T(8,128)S(1)}, u32[]{:S(2)}, u32[]{:S(2)}) async-start(f32[64,64,128]{2,1,0:T(8,128)} %bitcast.1), calls=%async_computation | async-start | bytes 4194304 | tf_op jit(solution)/shard_map/all_to_all | solution.py:339
  136.6 103.8 %copy-start.1 = (f32[4,2,2,128,128]{4,3,2,1,0:T(8,128)S(1)}, f32[4,2,2,128,128]{4,3,2,1,0:T(8,128)}, u32[]{:S(2)}) copy-start(f32[4,2,2,128,128]{4,3,2,1,0:T(8,128)} %copy-done) | copy-start | bytes 3145732
  136.6 103.8 %copy-start.6 = (bf16[2,2,256,256]{3,2,1,0:T(8,128)(2,1)S(1)}, bf16[2,2,256,256]{3,2,1,0:T(8,128)(2,1)}, u32[]{:S(2)}) copy-start(bf16[2,2,256,256]{3,2,1,0:T(8,128)(2,1)} %constant.66.clone.wyi) | copy-start | bytes 1572868
  136.6 103.8 %copy-start.9 = (bf16[2,256,256]{2,1,0:T(8,128)(2,1)S(1)}, bf16[2,256,256]{2,1,0:T(8,128)(2,1)}, u32[]{:S(2)}) copy-start(bf16[2,256,256]{2,1,0:T(8,128)(2,1)} %constant.64.clone.wzi) | copy-start | bytes 786436
  136.6 103.8 %copy-start.10 = (f32[2,128,128]{2,1,0:T(8,128)S(1)}, f32[2,128,128]{2,1,0:T(8,128)}, u32[]{:S(2)}) copy-start(f32[2,128,128]{2,1,0:T(8,128)} %fxc.3) | copy-start | bytes 393220
  240.4 8.3 %copy-start.3 = (f32[4,2,2,128,128]{4,3,2,1,0:T(8,128)S(1)}, f32[4,2,2,128,128]{4,3,2,1,0:T(8,128)}, u32[]{:S(2)}) copy-start(f32[4,2,2,128,128]{4,3,2,1,0:T(8,128)} %copy-done.2) | copy-start | bytes 3145732
  240.4 8.3 %copy-start.5 = (f32[4,2,2,128,128]{4,3,2,1,0:T(8,128)S(1)}, f32[4,2,2,128,128]{4,3,2,1,0:T(8,128)}, u32[]{:S(2)}) copy-start(f32[4,2,2,128,128]{4,3,2,1,0:T(8,128)} %copy-done.4) | copy-start | bytes 3145732
  241.9 8.5 %copy-start.14 = (s32[16]{0:T(128)S(1)}, s32[16]{0:T(128)}, u32[]{:S(2)}) copy-start(s32[16]{0:T(128)} %param.13) | copy-start | bytes 196
  241.9 10.5 %collective-permute-start.2 = (f32[4,2,2,128,128]{4,3,2,1,0:T(8,128)S(1)}, f32[4,2,2,128,128]{4,3,2,1,0:T(8,128)S(1)}, u32[]{:S(2)}, u32[]{:S(2)}) collective-permute-start(f32[4,2,2,128,128]{4,3,2,1,0:T(8,128)S(1)} %shard_map.102.rest_0_), channel_id=1, source_target_pairs={{0,64},{64,0},{1,65},{65,1},{2,66},{66,2},{3,67},{67,3},{4,68},{68... | collective-permute-start | bytes 3145736 | tf_op jit(solution)/shard_map/ppermute | solution.py:369
  250.2 2.8 %collective-permute-start.3 = (f32[4,2,2,128,128]{4,3,2,1,0:T(8,128)S(1)}, f32[4,2,2,128,128]{4,3,2,1,0:T(8,128)S(1)}, u32[]{:S(2)}, u32[]{:S(2)}) collective-permute-start(f32[4,2,2,128,128]{4,3,2,1,0:T(8,128)S(1)} %shard_map.103.rest_1_), channel_id=1, source_target_pairs={{0,64},{64,0},{1,65},{65,1},{2,66},{66,2},{3,67},{67,3},{4,68},{68... | collective-permute-start | bytes 3145736 | tf_op jit(solution)/shard_map/ppermute | solution.py:369

commit v8 on v7

--- a/solution.py
+++ b/solution.py
@@ -197,9 +197,8 @@
             out[x, pairs * step + m] = back[m, pl.ds(PITCH * x, 8), :]
 
 
-def backward_kernel(start, columns, wyi, wzi, fxc, own, arrived, out):
+def backward_pair(start, step, columns, wyi, wzi, fxc, own, arrived, out):
     n = fxc.shape[-1]
-    step = pl.program_id(0)
     place = start // 2 + step
     tiles = [jnp.concatenate([columns[:, j, a, place] for a in range(2)], axis=-1) for j in range(2)]
     lower = lax.broadcasted_iota(jnp.int32, tiles[0].shape, 1) < 4
@@ -215,6 +214,11 @@
         for r in range(2):
             part = x[2 * k * n : (2 * k + 2) * n, r * n : (r + 1) * n].reshape(2, n, n)
             out[2 * step + k, r] = part + fxc[...] * (own[2 * step + k, r] + arrived[2 * step + k, r])
+
+
+def backward_kernel(start, *refs):
+    for step in range(refs[-1].shape[0] // 2):
+        backward_pair(start, step, *refs)
 
 
 def place_kernel(pieces, slot, *rest):
@@ -341,10 +345,10 @@
     columns = pl.pallas_call(
         middle_kernel,
         out_shape=jax.ShapeDtypeStruct(columns.shape, F32),
-        grid=(mine // 4,),
+        grid=(1,),
         in_specs=[RESIDENT] * 4,
         out_specs=RESIDENT,
-        scratch_shapes=[pltpu.VMEM((2, n * PITCH, n), F32)] * 2,
+        scratch_shapes=[pltpu.VMEM((mine // 2, n * PITCH, n), F32)] * 2,
         compiler_params=limit(40),
         cost_estimate=taking(4),
         name="middle",
@@ -359,7 +363,7 @@
             pl.pallas_call(
                 functools.partial(backward_kernel, start),
                 out_shape=parts(count),
-                grid=(count // 2,),
+                grid=(1,),
                 in_specs=[RESIDENT] * 6,
                 out_specs=RESIDENT,
                 compiler_params=limit(40),

time: 255 us -> 255 us (level)
  no operation moved by 1% of the time
where the time goes in v8:
time: 255 us
  blocking collectives  104 us (41%)
  waiting for transfers between devices  94.2 us (37%)
  starting transfers between devices  37.6 us (15%)
  Pallas kernels  16.7 us (7%)
    all_to_all x1, blocking collectives, per_device(): lax.all_to_all(columns.reshape(flat), 'slab', split_axis=0, concat_axis=0...  104 us
    all_to_all x1, waiting for transfers between devices, per_device(): lax.all_to_all(spectrum.reshape(flat), 'slab', split_axis=0, concat_axis=...  93.2 us
    ppermute x2, starting transfers between devices, per_device(): arrived.append(lax.ppermute(sent, 'pool', swap))  20.7 us
    all_to_all x1, starting transfers between devices, per_device(): lax.all_to_all(spectrum.reshape(flat), 'slab', split_axis=0, concat_axis=...  9.91 us
    ppermute x2, starting transfers between devices, per_device(): others.append(lax.ppermute(results[-1], 'pool', swap))  6.99 us
  transfers between devices with their start and end apart: 5, of which 3 were waited for; matrix products, arithmetic and copies ran while one was open for 1% of the time, Pallas kernels for 3%

profile of v8, /device:TPU:33, one launch (start us, length us, event | category | flops | bytes accessed | tf_op | source)
XLA Modules:
  0.0 254.7 jit_solution(440775206357246888)
XLA Ops:
  0.0 1.2 shard_map.100.rest_0_
  1.3 20.5 %collective-permute-start = (f32[4,2,2,128,128]{4,3,2,1,0:T(8,128)S(1)}, f32[4,2,2,128,128]{4,3,2,1,0:T(8,128)S(1)}, u32[]{:S(2)}, u32[]{:S(2)}) collective-permute-start(f32[4,2,2,128,128]{4,3,2,1,0:T(8,128)S(1)} %shard_map.100.rest_0_), channel_id=1, source_target_pairs={{0,64},{64,0},{1,65},{65,1},{2,66},{66,2},{3,67},{67,3},{4,68},{68... | collective-permute-start | bytes 3145736 | tf_op jit(solution)/shard_map/ppermute | solution.py:307
  21.8 1.6 shard_map.101
  23.4 0.2 collective-permute-start.1
  23.6 0.5 collective-permute-done.arrived.refs_5_
  24.1 2.1 forward0.1
  26.2 2.9 %forward1.1 = f32[32,2,2,4,8,128]{5,4,3,2,1,0:T(8,128)} custom-call(f32[4,2,2,128,128]{4,3,2,1,0:T(8,128)S(1)} %get-tuple-element.10.own.refs_4_, f32[4,2,2,128,128]{4,3,2,1,0:T(8,128)S(1)} %collective-permute-done.1.arrived.refs_5_, bf16[2,256,256]{2,1,0:T(8,128)(2,1)S(1)} %copy-done.8, bf16[2,2,256,256]{3,2,1,0:T(8,128)(2,1)S(1)} %copy-done.7, ...), custom_call_target="tpu_custom_call" | custom-call | flops 240000000 | tf_op jit(solution)/shard_map/forward1/pallas_call | solution.py:324
  29.2 9.9 %all-to-all-start = ((f32[64,64,128]{2,1,0:T(8,128)}), f32[64,64,128]{2,1,0:T(8,128)S(1)}, u32[]{:S(2)}, u32[]{:S(2)}) async-start(f32[64,64,128]{2,1,0:T(8,128)} %bitcast.1), calls=%async_computation | async-start | bytes 4194304 | tf_op jit(solution)/shard_map/all_to_all | solution.py:343
  39.1 0.1 add.128
  39.2 0.1 convert_multiply_fusion
  39.3 0.7 copy.13
  40.0 0.1 broadcast_add_fusion
  40.0 1.0 fusion.kernel
  41.0 93.2 %all-to-all-done = f32[64,64,128]{2,1,0:T(8,128)S(1)} async-done(((f32[64,64,128]{2,1,0:T(8,128)}), f32[64,64,128]{2,1,0:T(8,128)S(1)}, u32[]{:S(2)}, u32[]{:S(2)}) %all-to-all-start) | async-done | bytes 2097184 | tf_op jit(solution)/shard_map/all_to_all | solution.py:343
  134.2 1.9 middle.1
  136.2 103.7 %all_to_all.10 = f32[64,64,128]{2,1,0:T(8,128)S(1)} all-to-all(f32[64,64,128]{2,1,0:T(8,128)S(1)} %bitcast.15), channel_id=1, replica_groups=mesh['group'=2,'pool'=2,'slab'=64] {'slab'}, dimensions={0} | all-to-all | bytes 4194304 | tf_op jit(solution)/shard_map/all_to_all | solution.py:356
  240.0 1.6 shard_map.102.rest_0_
  241.6 6.8 %collective-permute-start.2 = (f32[4,2,2,128,128]{4,3,2,1,0:T(8,128)S(1)}, f32[4,2,2,128,128]{4,3,2,1,0:T(8,128)S(1)}, u32[]{:S(2)}, u32[]{:S(2)}) collective-permute-start(f32[4,2,2,128,128]{4,3,2,1,0:T(8,128)S(1)} %shard_map.102.rest_0_), channel_id=1, source_target_pairs={{0,64},{64,0},{1,65},{65,1},{2,66},{66,2},{3,67},{67,3},{4,68},{68... | collective-permute-start | bytes 3145736 | tf_op jit(solution)/shard_map/ppermute | solution.py:373
  248.4 1.6 shard_map.103.rest_1_
  250.0 0.2 collective-permute-start.3
  250.2 0.1 select_reduce_fusion.slot
  250.3 1.9 shard_map.104.rest_2_
  252.2 0.6 collective-permute-done.3.rest_1_
  252.8 1.9 shard_map.105
  (36 shorter events, 0.1 us)
Async XLA Ops:
  1.2 22.9 %copy-start.7 = (bf16[2,2,256,256]{3,2,1,0:T(8,128)(2,1)S(1)}, bf16[2,2,256,256]{3,2,1,0:T(8,128)(2,1)}, u32[]{:S(2)}) copy-start(bf16[2,2,256,256]{3,2,1,0:T(8,128)(2,1)} %constant.65.clone.wy) | copy-start | bytes 1572868
  1.3 22.8 %copy-start.8 = (bf16[2,256,256]{2,1,0:T(8,128)(2,1)S(1)}, bf16[2,256,256]{2,1,0:T(8,128)(2,1)}, u32[]{:S(2)}) copy-start(bf16[2,256,256]{2,1,0:T(8,128)(2,1)} %constant.63.clone.wz) | copy-start | bytes 786436
  1.3 22.8 %collective-permute-start = (f32[4,2,2,128,128]{4,3,2,1,0:T(8,128)S(1)}, f32[4,2,2,128,128]{4,3,2,1,0:T(8,128)S(1)}, u32[]{:S(2)}, u32[]{:S(2)}) collective-permute-start(f32[4,2,2,128,128]{4,3,2,1,0:T(8,128)S(1)} %shard_map.100.rest_0_), channel_id=1, source_target_pairs={{0,64},{64,0},{1,65},{65,1},{2,66},{66,2},{3,67},{67,3},{4,68},{68... | collective-permute-start | bytes 3145736 | tf_op jit(solution)/shard_map/ppermute | solution.py:307
  23.4 2.8 %copy-start = (f32[4,2,2,128,128]{4,3,2,1,0:T(8,128)}, f32[4,2,2,128,128]{4,3,2,1,0:T(8,128)S(1)}, u32[]{:S(2)}) copy-start(f32[4,2,2,128,128]{4,3,2,1,0:T(8,128)S(1)} %get-tuple-element.9.own.refs_4_) | copy-start | bytes 3145732
  23.4 2.8 %collective-permute-start.1 = (f32[4,2,2,128,128]{4,3,2,1,0:T(8,128)S(1)}, f32[4,2,2,128,128]{4,3,2,1,0:T(8,128)S(1)}, u32[]{:S(2)}, u32[]{:S(2)}) collective-permute-start(f32[4,2,2,128,128]{4,3,2,1,0:T(8,128)S(1)} %get-tuple-element.11), channel_id=1, source_target_pairs={{0,64},{64,0},{1,65},{65,1},{2,66},{66,2},{3,67},{67,3},{4,68},{68... | collective-permute-start | bytes 3145736 | tf_op jit(solution)/shard_map/ppermute | solution.py:307
  26.2 2.9 %copy-start.4 = (f32[4,2,2,128,128]{4,3,2,1,0:T(8,128)}, f32[4,2,2,128,128]{4,3,2,1,0:T(8,128)S(1)}, u32[]{:S(2)}) copy-start(f32[4,2,2,128,128]{4,3,2,1,0:T(8,128)S(1)} %get-tuple-element.10.own.refs_4_) | copy-start | bytes 3145732
  26.2 2.9 %copy-start.2 = (f32[4,2,2,128,128]{4,3,2,1,0:T(8,128)}, f32[4,2,2,128,128]{4,3,2,1,0:T(8,128)S(1)}, u32[]{:S(2)}) copy-start(f32[4,2,2,128,128]{4,3,2,1,0:T(8,128)S(1)} %collective-permute-done.1.arrived.refs_5_) | copy-start | bytes 3145732
  29.1 10.1 %copy-start.13 = (s32[128,2,128]{2,1,0:T(2,128)S(1)}, s32[128,2,128]{2,1,0:T(2,128)}, u32[]{:S(2)}) copy-start(s32[128,2,128]{2,1,0:T(2,128)} %param.12) | copy-start | bytes 393220
  29.1 105.1 %copy-start.11 = (bf16[2,2,128,128]{3,2,1,0:T(8,128)(2,1)S(1)}, bf16[2,2,128,128]{3,2,1,0:T(8,128)(2,1)}, u32[]{:S(2)}) copy-start(bf16[2,2,128,128]{3,2,1,0:T(8,128)(2,1)} %constant.68.clone.wxi) | copy-start | bytes 393220
  29.1 105.1 %copy-start.12 = (bf16[2,2,128,128]{3,2,1,0:T(8,128)(2,1)S(1)}, bf16[2,2,128,128]{3,2,1,0:T(8,128)(2,1)}, u32[]{:S(2)}) copy-start(bf16[2,2,128,128]{3,2,1,0:T(8,128)(2,1)} %constant.67.clone.wx) | copy-start | bytes 393220
  29.2 105.1 %all-to-all-start = ((f32[64,64,128]{2,1,0:T(8,128)}), f32[64,64,128]{2,1,0:T(8,128)S(1)}, u32[]{:S(2)}, u32[]{:S(2)}) async-start(f32[64,64,128]{2,1,0:T(8,128)} %bitcast.1), calls=%async_computation | async-start | bytes 4194304 | tf_op jit(solution)/shard_map/all_to_all | solution.py:343
  136.2 103.8 %copy-start.1 = (f32[4,2,2,128,128]{4,3,2,1,0:T(8,128)S(1)}, f32[4,2,2,128,128]{4,3,2,1,0:T(8,128)}, u32[]{:S(2)}) copy-start(f32[4,2,2,128,128]{4,3,2,1,0:T(8,128)} %copy-done) | copy-start | bytes 3145732
  136.2 103.8 %copy-start.6 = (bf16[2,2,256,256]{3,2,1,0:T(8,128)(2,1)S(1)}, bf16[2,2,256,256]{3,2,1,0:T(8,128)(2,1)}, u32[]{:S(2)}) copy-start(bf16[2,2,256,256]{3,2,1,0:T(8,128)(2,1)} %constant.66.clone.refs_1_) | copy-start | bytes 1572868
  136.2 103.8 %copy-start.9 = (bf16[2,256,256]{2,1,0:T(8,128)(2,1)S(1)}, bf16[2,256,256]{2,1,0:T(8,128)(2,1)}, u32[]{:S(2)}) copy-start(bf16[2,256,256]{2,1,0:T(8,128)(2,1)} %constant.64.clone.refs_2_) | copy-start | bytes 786436
  136.2 103.8 %copy-start.10 = (f32[2,128,128]{2,1,0:T(8,128)S(1)}, f32[2,128,128]{2,1,0:T(8,128)}, u32[]{:S(2)}) copy-start(f32[2,128,128]{2,1,0:T(8,128)} %refs_3_.3) | copy-start | bytes 393220
  240.0 8.4 %copy-start.3 = (f32[4,2,2,128,128]{4,3,2,1,0:T(8,128)S(1)}, f32[4,2,2,128,128]{4,3,2,1,0:T(8,128)}, u32[]{:S(2)}) copy-start(f32[4,2,2,128,128]{4,3,2,1,0:T(8,128)} %copy-done.2) | copy-start | bytes 3145732
  240.0 8.4 %copy-start.5 = (f32[4,2,2,128,128]{4,3,2,1,0:T(8,128)S(1)}, f32[4,2,2,128,128]{4,3,2,1,0:T(8,128)}, u32[]{:S(2)}) copy-start(f32[4,2,2,128,128]{4,3,2,1,0:T(8,128)} %copy-done.4) | copy-start | bytes 3145732
  241.6 8.6 %copy-start.14 = (s32[16]{0:T(128)S(1)}, s32[16]{0:T(128)}, u32[]{:S(2)}) copy-start(s32[16]{0:T(128)} %param.13) | copy-start | bytes 196
  241.6 10.6 %collective-permute-start.2 = (f32[4,2,2,128,128]{4,3,2,1,0:T(8,128)S(1)}, f32[4,2,2,128,128]{4,3,2,1,0:T(8,128)S(1)}, u32[]{:S(2)}, u32[]{:S(2)}) collective-permute-start(f32[4,2,2,128,128]{4,3,2,1,0:T(8,128)S(1)} %shard_map.102.rest_0_), channel_id=1, source_target_pairs={{0,64},{64,0},{1,65},{65,1},{2,66},{66,2},{3,67},{67,3},{4,68},{68... | collective-permute-start | bytes 3145736 | tf_op jit(solution)/shard_map/ppermute | solution.py:373
  250.0 2.8 %collective-permute-start.3 = (f32[4,2,2,128,128]{4,3,2,1,0:T(8,128)S(1)}, f32[4,2,2,128,128]{4,3,2,1,0:T(8,128)S(1)}, u32[]{:S(2)}, u32[]{:S(2)}) collective-permute-start(f32[4,2,2,128,128]{4,3,2,1,0:T(8,128)S(1)} %shard_map.103.rest_1_), channel_id=1, source_target_pairs={{0,64},{64,0},{1,65},{65,1},{2,66},{66,2},{3,67},{67,3},{4,68},{68... | collective-permute-start | bytes 3145736 | tf_op jit(solution)/shard_map/ppermute | solution.py:373
